TPU v7x, 128 devices: a whole 4x4x4 slice. The times are simulated.
128 devices in a mesh: dp: 1, cp: 16 (over z, y), tp: 8 (over x, core).
Axes of the slice: x: 4, y: 4, z: 4, core: 2. Of those that a mesh axis runs over, the one named last changes fastest.
Arguments:
- x: bfloat16 [1, 16384, 4096], P('dp', ('cp', 'tp'))
- g_attn: bfloat16 [4096], replicated
- w_q: bfloat16 [4096, 32, 128], P(None, 'tp')
- w_k: bfloat16 [4096, 8, 128], P(None, 'tp')
- w_v: bfloat16 [4096, 8, 128], P(None, 'tp')
- w_o: bfloat16 [32, 128, 4096], P('tp')
- g_mlp: bfloat16 [4096], replicated
- w_gate: bfloat16 [4096, 14336], P(None, 'tp')
- w_up: bfloat16 [4096, 14336], P(None, 'tp')
- w_down: bfloat16 [14336, 4096], P('tp')
Outputs:
- output: bfloat16 [1, 16384, 4096], P('dp', ('cp', 'tp'))
All inputs are finite; a program needn't handle non-finite values.
Results may differ from a plain program's by a relative error of at most 0.02.
Values are sent between devices in bfloat16 or wider.
A program may use at most 1 GiB of HBM per device.

v0:
```python
import jax
import jax.numpy as jnp
from jax import lax
from jax.sharding import PartitionSpec as P

NORM_EPS = 1e-5
ROPE_THETA = 500000.0
TILE_ROWS = 256


def rms_norm(rows_in, gain_vec):
    rows_f32 = rows_in.astype(jnp.float32)
    mean_sq = jnp.mean(rows_f32 * rows_f32, axis=-1, keepdims=True)
    return (rows_f32 * lax.rsqrt(mean_sq + NORM_EPS) * gain_vec.astype(jnp.float32)).astype(jnp.bfloat16)


def apply_rope(heads_in, positions):
    head_dim = heads_in.shape[-1]
    half_dim = head_dim // 2
    inv_freq = ROPE_THETA ** (-2.0 * jnp.arange(half_dim, dtype=jnp.float32) / head_dim)
    angles = positions.astype(jnp.float32)[:, None] * inv_freq[None, :]
    angles = jnp.concatenate([angles, angles], axis=-1)[:, None, :]
    heads_f32 = heads_in.astype(jnp.float32)
    rotated = jnp.concatenate([-heads_f32[..., half_dim:], heads_f32[..., :half_dim]], axis=-1)
    return (heads_f32 * jnp.cos(angles) + rotated * jnp.sin(angles)).astype(jnp.bfloat16)


def stored_positions(row_ids, piece_len, cp_size):
    owner_cp = row_ids // (2 * piece_len)
    within = row_ids % (2 * piece_len)
    return jnp.where(within < piece_len, owner_cp * piece_len + within,
                     (2 * cp_size - 1 - owner_cp) * piece_len + within - piece_len)


def attend(q_rows, q_pos, keys, values, key_pos):
    q_len, n_kv_heads, group_size, head_dim = q_rows.shape
    n_tiles = max(1, q_len // TILE_ROWS)
    tile_len = q_len // n_tiles
    score_scale = head_dim ** -0.5

    def one_tile(tile_idx):
        row_start = tile_idx * tile_len
        q_tile = lax.dynamic_slice_in_dim(q_rows, row_start, tile_len, axis=0)
        pos_tile = lax.dynamic_slice_in_dim(q_pos, row_start, tile_len, axis=0)
        scores = jnp.einsum('qgrd,kgd->gqrk', q_tile, keys, preferred_element_type=jnp.float32) * score_scale
        visible = pos_tile[:, None, None] >= key_pos[None, None, :]
        scores = jnp.where(visible, scores, -1e30)
        weights = jnp.exp(scores - jnp.max(scores, axis=-1, keepdims=True))
        row_sum = jnp.sum(weights, axis=-1, keepdims=True)
        mixed_vals = jnp.einsum('gqrk,kgd->gqrd', weights.astype(jnp.bfloat16), values, preferred_element_type=jnp.float32) / row_sum
        return jnp.transpose(mixed_vals, (1, 0, 2, 3)).astype(jnp.bfloat16)

    tiles = lax.map(one_tile, jnp.arange(n_tiles))
    return tiles.reshape(q_len, n_kv_heads * group_size, head_dim)


def solution(mesh):
    cp_size = mesh.shape['cp']
    row_spec = P('dp', ('cp', 'tp'), None)
    head_cols = P(None, 'tp', None)

    def local_layer(x, g_attn, w_q, w_k, w_v, w_o, g_mlp, w_gate, w_up, w_down):
        x_rows = x[0]
        n_kv_local = w_k.shape[1]
        head_dim = w_q.shape[2]
        group_size = w_q.shape[1] // n_kv_local
        cp_index = lax.axis_index('cp')
        normed = lax.all_gather(rms_norm(x_rows, g_attn), 'tp', axis=0, tiled=True)
        seq_local = normed.shape[0]
        piece_len = seq_local // 2
        positions = stored_positions(cp_index * seq_local + jnp.arange(seq_local, dtype=jnp.int32), piece_len, cp_size)
        q_all = apply_rope(jnp.einsum('sd,dhk->shk', normed, w_q, preferred_element_type=jnp.float32).astype(jnp.bfloat16), positions)
        k_all = apply_rope(jnp.einsum('sd,dhk->shk', normed, w_k, preferred_element_type=jnp.float32).astype(jnp.bfloat16), positions)
        v_all = jnp.einsum('sd,dhk->shk', normed, w_v, preferred_element_type=jnp.float32).astype(jnp.bfloat16)
        k_seq = lax.all_gather(k_all, 'cp', axis=0, tiled=False)
        v_seq = lax.all_gather(v_all, 'cp', axis=0, tiled=False)
        key_pos = stored_positions(jnp.arange(cp_size * seq_local, dtype=jnp.int32), piece_len, cp_size).reshape(cp_size, seq_local)
        first_keys = k_seq[:, :piece_len].reshape(cp_size * piece_len, n_kv_local, head_dim)
        first_vals = v_seq[:, :piece_len].reshape(cp_size * piece_len, n_kv_local, head_dim)
        first_pos = key_pos[:, :piece_len].reshape(cp_size * piece_len)
        q_grp = q_all.reshape(seq_local, n_kv_local, group_size, head_dim)
        attn_first = attend(q_grp[:piece_len], positions[:piece_len], first_keys, first_vals, first_pos)
        attn_second = attend(q_grp[piece_len:], positions[piece_len:],
                             k_seq.reshape(cp_size * seq_local, n_kv_local, head_dim),
                             v_seq.reshape(cp_size * seq_local, n_kv_local, head_dim),
                             key_pos.reshape(cp_size * seq_local))
        attn_out = jnp.concatenate([attn_first, attn_second], axis=0)
        attn_part = jnp.einsum('shk,hkd->sd', attn_out, w_o, preferred_element_type=jnp.float32).astype(jnp.bfloat16)
        attn_rows = lax.psum_scatter(attn_part, 'tp', scatter_dimension=0, tiled=True)
        resid_rows = (x_rows.astype(jnp.float32) + attn_rows.astype(jnp.float32)).astype(jnp.bfloat16)
        normed_mlp = lax.all_gather(rms_norm(resid_rows, g_mlp), 'tp', axis=0, tiled=True)
        gate_proj = jnp.dot(normed_mlp, w_gate, preferred_element_type=jnp.float32)
        up_proj = jnp.dot(normed_mlp, w_up, preferred_element_type=jnp.float32)
        hidden = (jax.nn.silu(gate_proj) * up_proj).astype(jnp.bfloat16)
        down_part = jnp.dot(hidden, w_down, preferred_element_type=jnp.float32).astype(jnp.bfloat16)
        down_rows = lax.psum_scatter(down_part, 'tp', scatter_dimension=0, tiled=True)
        z_rows = (resid_rows.astype(jnp.float32) + down_rows.astype(jnp.float32)).astype(jnp.bfloat16)
        return z_rows[None]

    return jax.shard_map(local_layer, mesh=mesh,
                         in_specs=(row_spec, P(), head_cols, head_cols, head_cols, P('tp', None, None),
                                   P(), P(None, 'tp'), P(None, 'tp'), P('tp', None)),
                         out_specs=row_spec, check_vma=False)
```

profile of v0, /device:TPU:1, one launch (start us, length us, event | category | flops | bytes accessed | tf_op | source)
XLA Modules:
  0.0 699.4 jit_solution(5966489061327260467)
XLA Ops:
  11.6 53.0 %all-gather.7.cloned.1.call-done = bf16[1024,4096]{1,0:T(8,128)(2,1)} async-done(((bf16[128,4096]{1,0:T(8,128)(2,1)}), bf16[1024,4096]{1,0:T(8,128)(2,1)}) %all-gather.7.cloned.1.call-update) | async-done | bytes 8388624 | tf_op jit(solution)/shard_map/all_gather | solution.py:68
  64.6 6.3 fusion.95
  73.8 6.4 convolution_convert_fusion.1
  80.5 7.5 %copy.11 = bf16[4096,4,128]{0,2,1:T(8,128)(2,1)} copy(bf16[4096,4,128]{2,1,0:T(4,128)(2,1)} %param.16) | data formatting | bytes 8388608 | tf_op args[2]
  88.8 8.2 %fusion.117 = f32[1024,512]{0,1:S(1)} fusion(bf16[1024,4096]{1,0:T(8,128)(2,1)} %all-gather.7.cloned.1.call-done, bf16[4096,512]{0,1:T(8,128)(2,1)} %bitcast.149), kind=kOutput, calls=%fused_computation.135 | convolution fusion | flops 4294967296 | bytes 14680064
  99.0 25.7 %all-gather.11.cloned.1.call-done = bf16[16384,128]{0,1:T(8,128)(2,1)} async-done(((bf16[1024,128]{0,1:T(8,128)(2,1)}), bf16[16384,128]{0,1:T(8,128)(2,1)}) %all-gather.11.cloned.1.call-update) | async-done | bytes 4194320 | tf_op jit(solution)/shard_map/all_gather | solution.py:75
  124.7 4.9 copy.25
  133.0 44.6 %all-gather.13.cloned.1.call-done = bf16[16384,128]{1,0:T(8,128)(2,1)} async-done(((bf16[1024,128]{1,0:T(8,128)(2,1)}), bf16[16384,128]{1,0:T(8,128)(2,1)}) %all-gather.13.cloned.1.call-update) | async-done | bytes 4194320 | tf_op jit(solution)/shard_map/all_gather | solution.py:76
  180.9 97.8 %while.21 = (s32[]{:T(128)}, bf16[2,256,1,4,128]{4,1,0,3,2:T(8,128)(2,1)S(1)}, s32[2]{0:T(128)S(1)}, s32[512]{0:T(512)S(1)}, s32[16,512]{1,0:T(8,128)S(1)}, /*in...) while((s32[]{:T(128)}, ...), condition=%wide.region_4.5_spmd, body=%wide.region_1.4_spmd.sunk | while | flops 4389599232 | bytes 113892536 | solution.py:53
  183.7 15.8 %fusion.143 = (f32[256,4]{0,1:T(4,128)S(1)}, f32[256,4,8192]{2,0,1:T(8,128)}) fusion(pred[256,8192]{1,0:T(8,128)(4,1)S(1)} %broadcast_compare_fusion.5, bf16[8192,1,128]{2,0,1:T(8,128)(2,1)} %get-tuple-element.334, bf16[512,1,4,128]{0,3,2,1:T(8,128)(2,1)} %get-tuple-element.333, s32[]{:T(128)S(6)} %select_n.200), kind=kOutput, calls=%fused_computation.3.clone.1 | convolution fusion | flops 2172648448 | bytes 38014980 | tf_op jit(solution)/shard_map/while/body/eval_jaxpr/qgrd,kgd->gqrk/dot_general | solution.py:45
  199.5 15.1 %fusion.144 = f32[256,4]{0,1:T(4,128)S(1)} fusion(f32[256,4,8192]{2,0,1:T(8,128)} %get-tuple-element.260, f32[256,4]{0,1:T(4,128)S(1)} %get-tuple-element.261, pred[256,8192]{1,0:T(8,128)(4,1)S(1)} %broadcast_compare_fusion.5), kind=kLoop, calls=%fused_computation.4.clone.1 | loop fusion | flops 33553408 | bytes 35659776 | tf_op jit(solution)/shard_map/while/body/eval_jaxpr/reduce_sum | solution.py:49
  214.6 15.3 %fusion.145 = bf16[2,256,1,4,128]{4,1,0,3,2:T(8,128)(2,1)S(1)} fusion(bf16[2,256,1,4,128]{4,1,0,3,2:T(8,128)(2,1)S(1)} %get-tuple-element.317, s32[]{:T(128)} %get-tuple-element.316, bf16[8192,1,128]{2,0,1:T(8,128)(2,1)} %get-tuple-element.335, f32[256,4,8192]{2,0,1:T(8,128)} %get-tuple-element.260, f32[256,4]{0,1:T(4,128)S(1)} %get-tuple-element.261, ...), kind=kOutput, calls=%fused_computation.15.clone.1 | convolution fusion | flops 2181300224 | bytes 38019076 | tf_op jit(solution)/shard_map/while/body/eval_jaxpr/gqrk,kgd->gqrd/dot_general | solution.py:50
  232.4 15.8 %fusion.143 = (f32[256,4]{0,1:T(4,128)S(1)}, f32[256,4,8192]{2,0,1:T(8,128)}) fusion(pred[256,8192]{1,0:T(8,128)(4,1)S(1)} %broadcast_compare_fusion.5, bf16[8192,1,128]{2,0,1:T(8,128)(2,1)} %get-tuple-element.334, bf16[512,1,4,128]{0,3,2,1:T(8,128)(2,1)} %get-tuple-element.333, s32[]{:T(128)S(6)} %select_n.200), kind=kOutput, calls=%fused_computation.3.clone.1 | convolution fusion | flops 2172648448 | bytes 38014980 | tf_op jit(solution)/shard_map/while/body/eval_jaxpr/qgrd,kgd->gqrk/dot_general | solution.py:45
  248.2 15.1 %fusion.144 = f32[256,4]{0,1:T(4,128)S(1)} fusion(f32[256,4,8192]{2,0,1:T(8,128)} %get-tuple-element.260, f32[256,4]{0,1:T(4,128)S(1)} %get-tuple-element.261, pred[256,8192]{1,0:T(8,128)(4,1)S(1)} %broadcast_compare_fusion.5), kind=kLoop, calls=%fused_computation.4.clone.1 | loop fusion | flops 33553408 | bytes 35659776 | tf_op jit(solution)/shard_map/while/body/eval_jaxpr/reduce_sum | solution.py:49
  263.3 15.3 %fusion.145 = bf16[2,256,1,4,128]{4,1,0,3,2:T(8,128)(2,1)S(1)} fusion(bf16[2,256,1,4,128]{4,1,0,3,2:T(8,128)(2,1)S(1)} %get-tuple-element.317, s32[]{:T(128)} %get-tuple-element.316, bf16[8192,1,128]{2,0,1:T(8,128)(2,1)} %get-tuple-element.335, f32[256,4,8192]{2,0,1:T(8,128)} %get-tuple-element.260, f32[256,4]{0,1:T(4,128)S(1)} %get-tuple-element.261, ...), kind=kOutput, calls=%fused_computation.15.clone.1 | convolution fusion | flops 2181300224 | bytes 38019076 | tf_op jit(solution)/shard_map/while/body/eval_jaxpr/gqrk,kgd->gqrd/dot_general | solution.py:50
  278.7 6.6 copy.16
  285.4 171.2 %while.22 = (s32[]{:T(128)}, bf16[2,256,1,4,128]{4,1,0,3,2:T(8,128)(2,1)S(1)}, s32[2]{0:T(128)S(1)}, s32[512]{0:T(512)S(1)}, bf16[512,1,4,128]{0,3,2,1:T(8,128)(...) while((s32[]{:T(128)}, ...), condition=%wide.region_8.9_spmd.clone, body=%wide.region_5.8_spmd.clone.sunk | while | flops 8779266048 | bytes 227171504 | solution.py:53
  287.4 4.4 broadcast_compare_fusion.6
  291.7 28.4 %fusion.149 = (f32[256,4]{0,1:T(4,128)S(1)}, f32[256,4,16384]{2,0,1:T(8,128)}) fusion(pred[256,16384]{1,0:T(8,128)(4,1)} %broadcast_compare_fusion.6, bf16[16384,1,128]{2,0,1:T(8,128)(2,1)} %get-tuple-element.298, bf16[512,1,4,128]{0,3,2,1:T(8,128)(2,1)S(1)} %get-tuple-element.297, s32[]{:T(128)S(6)} %select_n.207), kind=kOutput, calls=%fused_computation.23.clone.1 | convolution fusion | flops 4345297920 | bytes 75763712 | tf_op jit(solution)/shard_map/while/body/eval_jaxpr/qgrd,kgd->gqrk/dot_general | solution.py:45
  320.1 22.8 %fusion.150 = f32[256,4]{0,1:T(4,128)S(1)} fusion(f32[256,4,16384]{2,0,1:T(8,128)} %get-tuple-element.269, f32[256,4]{0,1:T(4,128)S(1)} %get-tuple-element.270, pred[256,16384]{1,0:T(8,128)(4,1)} %broadcast_compare_fusion.6), kind=kLoop, calls=%fused_computation.24.clone.1 | loop fusion | flops 67107840 | bytes 71311360 | tf_op jit(solution)/shard_map/while/body/eval_jaxpr/reduce_sum | solution.py:49
  342.9 28.3 %fusion.151 = bf16[2,256,1,4,128]{4,1,0,3,2:T(8,128)(2,1)S(1)} fusion(bf16[2,256,1,4,128]{4,1,0,3,2:T(8,128)(2,1)S(1)} %get-tuple-element.283, s32[]{:T(128)} %get-tuple-element.282, bf16[16384,1,128]{2,0,1:T(8,128)(2,1)} %get-tuple-element.299, f32[256,4,16384]{2,0,1:T(8,128)} %get-tuple-element.269, f32[256,4]{0,1:T(4,128)S(1)} %get-tuple-element.270, ...), kind=kOutput, calls=%fused_computation.35.clone.1 | convolution fusion | flops 4362338304 | bytes 75767808 | tf_op jit(solution)/shard_map/while/body/eval_jaxpr/gqrk,kgd->gqrd/dot_general | solution.py:50
  372.7 4.4 broadcast_compare_fusion.6
  377.0 28.4 %fusion.149 = (f32[256,4]{0,1:T(4,128)S(1)}, f32[256,4,16384]{2,0,1:T(8,128)}) fusion(pred[256,16384]{1,0:T(8,128)(4,1)} %broadcast_compare_fusion.6, bf16[16384,1,128]{2,0,1:T(8,128)(2,1)} %get-tuple-element.298, bf16[512,1,4,128]{0,3,2,1:T(8,128)(2,1)S(1)} %get-tuple-element.297, s32[]{:T(128)S(6)} %select_n.207), kind=kOutput, calls=%fused_computation.23.clone.1 | convolution fusion | flops 4345297920 | bytes 75763712 | tf_op jit(solution)/shard_map/while/body/eval_jaxpr/qgrd,kgd->gqrk/dot_general | solution.py:45
  405.5 22.8 %fusion.150 = f32[256,4]{0,1:T(4,128)S(1)} fusion(f32[256,4,16384]{2,0,1:T(8,128)} %get-tuple-element.269, f32[256,4]{0,1:T(4,128)S(1)} %get-tuple-element.270, pred[256,16384]{1,0:T(8,128)(4,1)} %broadcast_compare_fusion.6), kind=kLoop, calls=%fused_computation.24.clone.1 | loop fusion | flops 67107840 | bytes 71311360 | tf_op jit(solution)/shard_map/while/body/eval_jaxpr/reduce_sum | solution.py:49
  428.2 28.3 %fusion.151 = bf16[2,256,1,4,128]{4,1,0,3,2:T(8,128)(2,1)S(1)} fusion(bf16[2,256,1,4,128]{4,1,0,3,2:T(8,128)(2,1)S(1)} %get-tuple-element.283, s32[]{:T(128)} %get-tuple-element.282, bf16[16384,1,128]{2,0,1:T(8,128)(2,1)} %get-tuple-element.299, f32[256,4,16384]{2,0,1:T(8,128)} %get-tuple-element.269, f32[256,4]{0,1:T(4,128)S(1)} %get-tuple-element.270, ...), kind=kOutput, calls=%fused_computation.35.clone.1 | convolution fusion | flops 4362338304 | bytes 75767808 | tf_op jit(solution)/shard_map/while/body/eval_jaxpr/gqrk,kgd->gqrd/dot_general | solution.py:50
  456.6 9.8 %bitcast_convert_fusion = bf16[1024,4096]{1,0:T(8,128)(2,1)} fusion(bf16[4,128,4096]{2,1,0:T(8,128)(2,1)} %param.19, bf16[512,4,128]{2,0,1:T(8,128)(2,1)S(1)} %bitcast.156, bf16[512,4,128]{2,0,1:T(8,128)(2,1)S(1)} %bitcast.157), kind=kOutput, calls=%fused_computation.60 | convolution fusion | flops 4301258752 | bytes 13631488 | tf_op jit(solution)/shard_map/shk,hkd->sd/dot_general | solution.py:88
  467.1 51.3 %reduce-scatter.3.cloned.1.call-done = bf16[128,4096]{1,0:T(8,128)(2,1)} async-done(((bf16[1024,4096]{1,0:T(8,128)(2,1)}), bf16[128,4096]{1,0:T(8,128)(2,1)}) %reduce-scatter.3.cloned.1.call-update) | async-done | bytes 1048592 | tf_op jit(solution)/shard_map/reduce_scatter | solution.py:89
  522.7 50.1 %all-gather.9.cloned.1.call-done = bf16[1024,4096]{1,0:T(8,128)(2,1)} async-done(((bf16[128,4096]{1,0:T(8,128)(2,1)}), bf16[1024,4096]{1,0:T(8,128)(2,1)}) %all-gather.9.cloned.1.call-update) | async-done | bytes 8388624 | tf_op jit(solution)/shard_map/all_gather | solution.py:91
  572.8 21.8 %fusion.118 = f32[1024,1792]{1,0:T(8,128)} fusion(bf16[1024,4096]{1,0:T(8,128)(2,1)} %all-gather.9.cloned.1.call-done, bf16[4096,1792]{1,0:T(8,128)(2,1)} %param.21), kind=kOutput, calls=%fused_computation.136 | convolution fusion | flops 15032385536 | bytes 30408704 | tf_op jit(solution)/shard_map/dot_general | solution.py:92
  594.6 23.5 %multiply_convert_fusion = bf16[1024,1792]{1,0:T(8,128)(2,1)} fusion(f32[1024,1792]{1,0:T(8,128)} %fusion.118, bf16[1024,4096]{1,0:T(8,128)(2,1)} %all-gather.9.cloned.1.call-done, bf16[4096,1792]{1,0:T(8,128)(2,1)} %param.22), kind=kOutput, calls=%fused_computation.62 | convolution fusion | flops 15043395584 | bytes 34078720 | tf_op jit(solution)/shard_map/dot_general | solution.py:93
  618.1 19.5 %convolution_convert_fusion = bf16[1024,4096]{1,0:T(8,128)(2,1)} fusion(bf16[1024,1792]{1,0:T(8,128)(2,1)} %multiply_convert_fusion, bf16[1792,4096]{1,0:T(8,128)(2,1)S(1)} %bitcast.159), kind=kOutput, calls=%fused_computation.61 | convolution fusion | flops 15036579840 | bytes 26738688 | tf_op jit(solution)/shard_map/dot_general | solution.py:95
  637.7 52.0 %reduce-scatter.5.cloned.1.call-done = bf16[128,4096]{1,0:T(8,128)(2,1)} async-done(((bf16[1024,4096]{1,0:T(8,128)(2,1)}), bf16[128,4096]{1,0:T(8,128)(2,1)}) %reduce-scatter.5.cloned.1.call-update) | async-done | bytes 1048592 | tf_op jit(solution)/shard_map/reduce_scatter | solution.py:96
  (86 shorter events, 30.6 us)
Async XLA Ops:
  6.5 58.1 %copy-start = (bf16[4096,1,128]{2,0,1:T(8,128)(2,1)S(1)}, bf16[4096,1,128]{2,0,1:T(8,128)(2,1)}, u32[]{:S(2)}) copy-start(bf16[4096,1,128]{2,0,1:T(8,128)(2,1)} %param.17) | copy-start | bytes 3145732
  6.5 58.1 %all-gather.7.cloned.1.call-start = ((), (), s32[]{:S(2)}) async-start(), calls=%async_computation.2 | async-start | bytes 9437184 | tf_op jit(solution)/shard_map/all_gather | solution.py:68
  11.4 113.3 %all-gather.11.cloned.1.call-start = ((), (), s32[]{:S(2)}) async-start(), calls=%async_computation.6 | async-start | bytes 4456448 | tf_op jit(solution)/shard_map/all_gather | solution.py:75
  11.6 62.2 %copy-start.9 = (bf16[4096,1,128]{2,0,1:T(8,128)(2,1)S(1)}, bf16[4096,1,128]{2,0,1:T(8,128)(2,1)}, u32[]{:S(2)}) copy-start(bf16[4096,1,128]{2,0,1:T(8,128)(2,1)} %param.18) | copy-start | bytes 3145732
  73.7 103.9 %all-gather.13.cloned.1.call-start = ((), (), s32[]{:S(2)}) async-start(), calls=%async_computation.7 | async-start | bytes 4456448 | tf_op jit(solution)/shard_map/all_gather | solution.py:76
  80.2 438.1 %reduce-scatter.3.cloned.1.call-start = ((), (), s32[]{:S(2)}) async-start(), calls=%async_computation.3 | async-start | bytes 9437184 | tf_op jit(solution)/shard_map/reduce_scatter | solution.py:89
  278.7 6.7 copy-start.4
  278.7 6.7 copy-start.6
  278.7 6.7 copy-start.7
  285.4 171.2 %copy-start.5 = (bf16[2,256,1,4,128]{4,1,0,3,2:T(8,128)(2,1)S(1)}, bf16[2,256,1,4,128]{4,1,0,3,2:T(8,128)(2,1)}, u32[]{:S(2)}) copy-start(bf16[2,256,1,4,128]{4,1,0,3,2:T(8,128)(2,1)} %copy-done.4) | copy-start | bytes 1572868
  466.4 0.7 copy-start.8
  466.4 52.0 %copy-start.2 = (bf16[1,128,4096]{2,1,0:T(8,128)(2,1)S(1)}, bf16[1,128,4096]{2,1,0:T(8,128)(2,1)}, u32[]{:S(2)}) copy-start(bf16[1,128,4096]{2,1,0:T(8,128)(2,1)} %param.14) | copy-start | bytes 3145732
  466.4 106.4 %all-gather.9.cloned.1.call-start = ((), (), s32[]{:S(2)}) async-start(), calls=%async_computation.4 | async-start | bytes 9437184 | tf_op jit(solution)/shard_map/all_gather | solution.py:91
  522.6 167.1 %reduce-scatter.5.cloned.1.call-start = ((), (), s32[]{:S(2)}) async-start(), calls=%async_computation.5 | async-start | bytes 9437184 | tf_op jit(solution)/shard_map/reduce_scatter | solution.py:96
  572.8 45.3 %slice-start = ((s8[14680064]{0:T(1024)(128)(4,1)}), s8[4194304]{0:T(1024)(128)(4,1)S(1)}, s32[]{:S(2)}) async-start(s8[14680064]{0:T(1024)(128)(4,1)} %bitcast.158), calls=%async_computation.8 | async-start | bytes 8388608
  572.8 45.3 %slice-start.1 = ((s8[14680064]{0:T(1024)(128)(4,1)}), s8[4194304]{0:T(1024)(128)(4,1)S(1)}, s32[]{:S(2)}) async-start(s8[14680064]{0:T(1024)(128)(4,1)} %bitcast.158), calls=%async_computation.9 | async-start | bytes 8388608
  594.6 23.5 %slice-start.2 = ((s8[14680064]{0:T(1024)(128)(4,1)}), s8[4194304]{0:T(1024)(128)(4,1)S(1)}, s32[]{:S(2)}) async-start(s8[14680064]{0:T(1024)(128)(4,1)} %bitcast.158), calls=%async_computation.10 | async-start | bytes 8388608
  594.6 23.5 %slice-start.3 = ((s8[14680064]{0:T(1024)(128)(4,1)}), s8[2097152]{0:T(1024)(128)(4,1)S(1)}, s32[]{:S(2)}) async-start(s8[14680064]{0:T(1024)(128)(4,1)} %bitcast.158), calls=%async_computation.11 | async-start | bytes 4194304
  618.1 74.3 %copy-start.1 = (bf16[4096,1,128]{2,0,1:T(8,128)(2,1)S(1)}, bf16[4096,1,128]{2,0,1:T(8,128)(2,1)}, u32[]{:S(2)}) copy-start(bf16[4096,1,128]{2,0,1:T(8,128)(2,1)} %param.17) | copy-start | bytes 3145732
  637.6 52.1 %copy-start.3 = (bf16[128,4096]{1,0:T(8,128)(2,1)S(1)}, bf16[128,4096]{1,0:T(8,128)(2,1)}, u32[]{:S(2)}) copy-start(bf16[128,4096]{1,0:T(8,128)(2,1)} %reduce-scatter.3.cloned.1.call-done) | copy-start | bytes 3145732
Sparse Core Ops, SparseCore 0:
  11.5 53.0 all-gather.6
  73.8 50.8 all-gather.10
  126.8 50.7 all-gather.12
  466.5 51.7 reduce-scatter.2
  522.8 50.0 all-gather.8
  637.8 51.8 reduce-scatter.4
where the time goes:
time: 705 us; the launch traced here: 699 us
  waiting for transfers between devices  277 us (39%)
  matrix products  271 us (38%)
  other arithmetic  103 us (15%)
  local copies, waits for them, and re-layouts  30.9 us (4%)
  between operations  13.9 us (2%)
    dot_general x4, matrix products, one_tile(): jnp.einsum('qgrd,kgd->gqrk', q_tile, keys, preferred_element_type=jnp.flo...  88.4 us
    dot_general x4, matrix products, one_tile(): jnp.einsum('gqrk,kgd->gqrd', weights.astype(jnp.bfloat16), values, prefer...  87.3 us
    reduce_sum x4, other arithmetic, one_tile(): row_sum = jnp.sum(weights, axis=-1, keepdims=True)  75.7 us
    all_gather x1, waiting for transfers between devices, local_layer(): normed = lax.all_gather(rms_norm(x_rows, g_attn), 'tp', axis=0, tiled=True)  53 us
    reduce_scatter x1, waiting for transfers between devices, local_layer(): lax.psum_scatter(down_part, 'tp', scatter_dimension=0, tiled=True)  52 us
    reduce_scatter x1, waiting for transfers between devices, local_layer(): lax.psum_scatter(attn_part, 'tp', scatter_dimension=0, tiled=True)  51.3 us
    all_gather x1, waiting for transfers between devices, local_layer(): lax.all_gather(rms_norm(resid_rows, g_mlp), 'tp', axis=0, tiled=True)  50.1 us
    all_gather x1, waiting for transfers between devices, local_layer(): v_seq = lax.all_gather(v_all, 'cp', axis=0, tiled=False)  44.6 us
  transfers between devices with their start and end apart: 6, of which 6 were waited for; matrix products, arithmetic and copies ran while one was open for 5% of the time, Pallas kernels for 0%

commit v1 on v0

v1 whole, which is shorter than its diff:
```python
import functools
import math
import jax
import jax.numpy as jnp
from jax import lax
from jax.experimental import pallas as pl
from jax.experimental.pallas import tpu as pltpu
from jax.sharding import PartitionSpec as P

NORM_EPS = 1e-5
ROPE_THETA = 500000.0
CP = 16
PIECE = 512
HD = 128


def rms_norm(rows_in, gain_vec):
    rows_f32 = rows_in.astype(jnp.float32)
    mean_sq = jnp.mean(rows_f32 * rows_f32, axis=-1, keepdims=True)
    return (rows_f32 * lax.rsqrt(mean_sq + NORM_EPS) * gain_vec.astype(jnp.float32)).astype(jnp.bfloat16)


def rope_tables(positions):
    inv_freq = ROPE_THETA ** (-2.0 * jnp.arange(HD // 2, dtype=jnp.float32) / HD)
    angles = positions.astype(jnp.float32)[:, None] * inv_freq[None, :]
    c, s = jnp.cos(angles), jnp.sin(angles)
    return jnp.concatenate([c, c], axis=-1), jnp.concatenate([-s, s], axis=-1)


def rope(v, cos, sin):
    f = v.astype(jnp.float32)
    swapped = jnp.concatenate([f[..., HD // 2:], f[..., :HD // 2]], axis=-1)
    return (f * cos + swapped * sin).astype(jnp.bfloat16)


def flash_kernel(n_heads, q_ref, k_ref, v_ref, o_ref, m_ref, l_ref, acc_ref):
    me = lax.axis_index('cp')
    scale = HD ** -0.5 * math.log2(math.e)

    def block(q_row, src, kv_row, masked):
        k = k_ref[src, pl.ds(kv_row, PIECE), :]
        v = v_ref[src, pl.ds(kv_row, PIECE), :]
        for h in range(n_heads):
            cols = slice(h * HD, (h + 1) * HD)
            q = q_ref[q_row:q_row + PIECE, cols]
            s = lax.dot_general(q, k, (((1,), (1,)), ((), ())), preferred_element_type=jnp.float32) * scale
            if masked:
                row = lax.broadcasted_iota(jnp.int32, (PIECE, PIECE), 0)
                col = lax.broadcasted_iota(jnp.int32, (PIECE, PIECE), 1)
                s = jnp.where(row >= col, s, -1e30)
            m_old = m_ref[:, cols]
            m_new = jnp.maximum(m_old, jnp.max(s, axis=1, keepdims=True))
            alpha = jnp.exp2(m_old - m_new)
            p = [jnp.exp2(s[:, i * HD:(i + 1) * HD] - m_new) for i in range(PIECE // HD)]
            psum = p[0]
            for part in p[1:]:
                psum = psum + part
            l_ref[:, cols] = l_ref[:, cols] * alpha + psum
            pb = jnp.concatenate([part.astype(jnp.bfloat16) for part in p], axis=1)
            pv = jnp.dot(pb, v, preferred_element_type=jnp.float32)
            acc_ref[:, cols] = acc_ref[:, cols] * alpha + pv
            m_ref[:, cols] = m_new

    for half in range(2):
        q_row = half * PIECE
        m_ref[...] = jnp.full_like(m_ref, -1e30)
        l_ref[...] = jnp.zeros_like(l_ref)
        acc_ref[...] = jnp.zeros_like(acc_ref)
        n_low = me if half == 0 else CP

        @pl.loop(0, n_low)
        def _(j):
            block(q_row, j, 0, False)

        if half == 1:
            @pl.loop(me + 1, CP)
            def _(j):
                block(q_row, j, PIECE, False)

        block(q_row, me, q_row, True)
        for h in range(n_heads):
            cols = slice(h * HD, (h + 1) * HD)
            total = jnp.sum(l_ref[:, cols], axis=1, keepdims=True)
            o_ref[q_row:q_row + PIECE, cols] = (acc_ref[:, cols] / total).astype(jnp.bfloat16)


def flash(q, k, v):
    rows, width = q.shape
    vmem = pl.BlockSpec(memory_space=pltpu.VMEM)
    return pl.pallas_call(
        functools.partial(flash_kernel, width // HD),
        out_shape=jax.ShapeDtypeStruct((rows, width), jnp.bfloat16),
        in_specs=[vmem] * 3,
        out_specs=vmem,
        scratch_shapes=[pltpu.VMEM((PIECE, width), jnp.float32)] * 3,
        compiler_params=pltpu.CompilerParams(vmem_limit_bytes=50 * 2 ** 20),
        cost_estimate=pl.CostEstimate(flops=18 * 10 ** 9, bytes_accessed=10 * 2 ** 20, transcendentals=35 * 10 ** 6),
    )(q, k, v)


def solution(mesh):
    row_spec = P('dp', ('cp', 'tp'), None)
    head_cols = P(None, 'tp', None)

    def local_layer(x, g_attn, w_q, w_k, w_v, w_o, g_mlp, w_gate, w_up, w_down):
        x_rows = x[0]
        cp_index = lax.axis_index('cp')
        normed = lax.all_gather(rms_norm(x_rows, g_attn), 'tp', axis=0, tiled=True)
        rows = normed.shape[0]
        j = jnp.arange(rows, dtype=jnp.int32)
        positions = jnp.where(j < PIECE, cp_index * PIECE + j, (2 * CP - 1 - cp_index) * PIECE + j - PIECE)
        cos, sin = rope_tables(positions)
        n_heads = w_q.shape[1]
        dim = w_q.shape[0]
        q = jnp.dot(normed, w_q.reshape(dim, n_heads * HD), preferred_element_type=jnp.float32).astype(jnp.bfloat16)
        q = rope(q.reshape(rows, n_heads, HD), cos[:, None], sin[:, None]).reshape(rows, n_heads * HD)
        k = rope(jnp.dot(normed, w_k.reshape(dim, HD), preferred_element_type=jnp.float32).astype(jnp.bfloat16), cos, sin)
        v = jnp.dot(normed, w_v.reshape(dim, HD), preferred_element_type=jnp.float32).astype(jnp.bfloat16)
        k_seq = lax.all_gather(k, 'cp', axis=0, tiled=False)
        v_seq = lax.all_gather(v, 'cp', axis=0, tiled=False)
        attn_out = flash(q, k_seq, v_seq)
        attn_part = jnp.dot(attn_out, w_o.reshape(n_heads * HD, dim), preferred_element_type=jnp.float32).astype(jnp.bfloat16)
        attn_rows = lax.psum_scatter(attn_part, 'tp', scatter_dimension=0, tiled=True)
        resid_rows = (x_rows.astype(jnp.float32) + attn_rows.astype(jnp.float32)).astype(jnp.bfloat16)
        normed_mlp = lax.all_gather(rms_norm(resid_rows, g_mlp), 'tp', axis=0, tiled=True)
        gate_proj = jnp.dot(normed_mlp, w_gate, preferred_element_type=jnp.float32)
        up_proj = jnp.dot(normed_mlp, w_up, preferred_element_type=jnp.float32)
        hidden = (jax.nn.silu(gate_proj) * up_proj).astype(jnp.bfloat16)
        down_part = jnp.dot(hidden, w_down, preferred_element_type=jnp.float32).astype(jnp.bfloat16)
        down_rows = lax.psum_scatter(down_part, 'tp', scatter_dimension=0, tiled=True)
        z_rows = (resid_rows.astype(jnp.float32) + down_rows.astype(jnp.float32)).astype(jnp.bfloat16)
        return z_rows[None]

    return jax.shard_map(local_layer, mesh=mesh,
                         in_specs=(row_spec, P(), head_cols, head_cols, head_cols, P('tp', None, None),
                                   P(), P(None, 'tp'), P(None, 'tp'), P('tp', None)),
                         out_specs=row_spec, check_vma=False)
```

time: 705 us -> 488 us (0.69)
  matrix products: 271 us -> 94.5 us
  other arithmetic: 103 us -> 15.7 us
  Pallas kernels: 0 us -> 67.2 us
  local copies, waits for them, and re-layouts: 30.9 us -> 12.1 us
    dot_general x11 -> x4, matrix products: 198 us -> 29.8 us  [the longest x1 10.4 us: local_layer(): jnp.dot(normed, w_q.reshape(dim, n_heads * HD), preferred_element_type=jn...]
    reduce_sum x4 -> x0, other arithmetic: 75.7 us -> none  [one_tile(): row_sum = jnp.sum(weights, axis=-1, keepdims=True)]
    pallas_call x0 -> x1, Pallas kernels: none -> 67.2 us  [flash(): pl.pallas_call(functools.partial(flash_kernel, width // HD), out_shape=ja...]
    unnamed x31 -> x26, local copies, waits for them, and re-layouts: 19.8 us -> 0.99 us
    ge x4 -> x0, other arithmetic: 11.1 us -> none  [one_tile(): visible = pos_tile[:, None, None] >= key_pos[None, None, :]]
    unnamed x1 -> x0, matrix products: 8.23 us -> none
  transfers between devices with their start and end apart: 6 -> 6, of which waited for: 6 -> 6; matrix products, arithmetic and copies ran while one was open for 5% -> 6% of each run, Pallas kernels for 0% -> 0%
where the time goes in v1:
time: 488 us; the launch traced here: 483 us
  waiting for transfers between devices  279 us (57%)
  matrix products  94.5 us (19%)
  Pallas kernels  67.2 us (14%)
  other arithmetic  15.7 us (3%)
  between operations  14.1 us (3%)
  local copies, waits for them, and re-layouts  12.1 us (2%)
    pallas_call x1, Pallas kernels, flash(): pl.pallas_call(functools.partial(flash_kernel, width // HD), out_shape=ja...  67.2 us
    all_gather x1, waiting for transfers between devices, local_layer(): normed = lax.all_gather(rms_norm(x_rows, g_attn), 'tp', axis=0, tiled=True)  52.1 us
    reduce_scatter x1, waiting for transfers between devices, local_layer(): lax.psum_scatter(down_part, 'tp', scatter_dimension=0, tiled=True)  52 us
    reduce_scatter x1, waiting for transfers between devices, local_layer(): lax.psum_scatter(attn_part, 'tp', scatter_dimension=0, tiled=True)  51.3 us
    all_gather x1, waiting for transfers between devices, local_layer(): lax.all_gather(rms_norm(resid_rows, g_mlp), 'tp', axis=0, tiled=True)  49.9 us
    all_gather x1, waiting for transfers between devices, local_layer(): v_seq = lax.all_gather(v, 'cp', axis=0, tiled=False)  46.6 us
    all_gather x1, waiting for transfers between devices, local_layer(): k_seq = lax.all_gather(k, 'cp', axis=0, tiled=False)  26.7 us
    dot_general x1, matrix products, local_layer(): up_proj = jnp.dot(normed_mlp, w_up, preferred_element_type=jnp.float32)  23.5 us
  transfers between devices with their start and end apart: 6, of which 6 were waited for; matrix products, arithmetic and copies ran while one was open for 6% of the time, Pallas kernels for 0%

profile of v1, /device:TPU:1, one launch (start us, length us, event | category | flops | bytes accessed | tf_op | source)
XLA Modules:
  0.0 483.0 jit_solution(18220534248429679044)
XLA Ops:
  6.5 1.6 fusion.7
  8.2 0.7 convert_element_type.81
  8.9 2.5 fusion.9
  11.5 1.0 multiply_cosine_fusion
  12.5 52.1 %all-gather.7.cloned.1.call-done = bf16[1024,4096]{1,0:T(8,128)(2,1)} async-done(((bf16[128,4096]{1,0:T(8,128)(2,1)}), bf16[1024,4096]{1,0:T(8,128)(2,1)}) %all-gather.7.cloned.1.call-update) | async-done | bytes 8388624 | tf_op jit(solution)/shard_map/all_gather | solution.py:108
  64.6 6.3 %fusion.18 = f32[1024,128]{0,1:T(8,128)S(1)} fusion(bf16[1024,4096]{1,0:T(8,128)(2,1)} %all-gather.7.cloned.1.call-done, bf16[4096,1,128]{2,0,1:T(8,128)(2,1)S(1)} %copy-done), kind=kOutput, calls=%fused_computation.28 | convolution fusion | flops 1074003968 | bytes 9961472 | tf_op jit(solution)/shard_map/dot_general | solution.py:117
  71.0 0.9 fusion.23
  71.9 0.3 copy-done.8
  72.2 6.4 %convolution_convert_fusion.2 = bf16[1024,128]{1,0:T(8,128)(2,1)} fusion(bf16[1024,4096]{1,0:T(8,128)(2,1)} %all-gather.7.cloned.1.call-done, bf16[4096,1,128]{2,0,1:T(8,128)(2,1)S(1)} %copy-done.8), kind=kOutput, calls=%fused_computation.26 | convolution fusion | flops 1073872896 | bytes 9699328 | tf_op jit(solution)/shard_map/dot_general | solution.py:118
  78.9 1.0 copy.13
  80.1 10.4 %fusion.15 = f32[1024,512]{1,0:T(8,128)} fusion(bf16[1024,4096]{1,0:T(8,128)(2,1)} %all-gather.7.cloned.1.call-done, bf16[512,8,4,128]{3,2,1,0:T(4,128)(2,1)} %bitcast.56), kind=kOutput, calls=%fused_computation.25 | convolution fusion | flops 4296015872 | bytes 14680064 | tf_op jit(solution)/shard_map/dot_general | solution.py:115
  90.5 1.9 reshape.63
  92.4 1.2 fusion.25
  93.6 1.2 maximum_multiply_fusion
  94.9 0.4 mul.106
  95.3 0.8 fusion.11.q_ref
  96.1 26.7 %all-gather.11.cloned.1.call-done = bf16[16384,128]{0,1:T(8,128)(2,1)} async-done(((bf16[1024,128]{0,1:T(8,128)(2,1)}), bf16[16384,128]{0,1:T(8,128)(2,1)}) %all-gather.11.cloned.1.call-update) | async-done | bytes 4194320 | tf_op jit(solution)/shard_map/all_gather | solution.py:119
  122.8 6.4 %copy.14 = bf16[16384,128]{1,0:T(8,128)(2,1)} copy(bf16[16384,128]{0,1:T(8,128)(2,1)} %all-gather.11.cloned.1.call-done) | data formatting | bytes 8388608 | tf_op jit(solution)/shard_map/all_gather | solution.py:119
  129.2 46.6 %all-gather.13.cloned.1.call-done = bf16[16384,128]{1,0:T(8,128)(2,1)} async-done(((bf16[1024,128]{1,0:T(8,128)(2,1)}), bf16[16384,128]{1,0:T(8,128)(2,1)}) %all-gather.13.cloned.1.call-update) | async-done | bytes 4194320 | tf_op jit(solution)/shard_map/all_gather | solution.py:120
  175.8 67.2 %shard_map.100 = bf16[1024,512]{1,0:T(8,128)(2,1)S(1)} custom-call(bf16[1024,512]{1,0:T(8,128)(2,1)S(1)} %fusion.11.q_ref, bf16[16,1024,128]{2,1,0:T(8,128)(2,1)} %bitcast.53, bf16[16,1024,128]{2,1,0:T(8,128)(2,1)} %bitcast.58), custom_call_target="tpu_custom_call" | custom-call | flops 17999998976 | bytes 10485760 | tf_op jit(solution)/shard_map/pallas_call | solution.py:90
  243.0 6.7 %convolution_convert_fusion.1 = bf16[1024,4096]{1,0:T(8,128)(2,1)} fusion(bf16[1024,512]{1,0:T(8,128)(2,1)S(1)} %shard_map.100, bf16[512,4096]{1,0:T(8,128)(2,1)S(1)} %bitcast.57), kind=kOutput, calls=%fused_computation.1 | convolution fusion | flops 4299161600 | bytes 13631488 | tf_op jit(solution)/shard_map/dot_general | solution.py:122
  249.8 0.6 copy-done.6
  250.4 51.3 %reduce-scatter.3.cloned.1.call-done = bf16[128,4096]{1,0:T(8,128)(2,1)} async-done(((bf16[1024,4096]{1,0:T(8,128)(2,1)}), bf16[128,4096]{1,0:T(8,128)(2,1)}) %reduce-scatter.3.cloned.1.call-update) | async-done | bytes 1048592 | tf_op jit(solution)/shard_map/reduce_scatter | solution.py:123
  301.8 1.6 fusion.3
  303.4 2.6 fusion.5
  306.1 0.3 reduce-scatter.5.cloned.1.call-start
  306.4 49.9 %all-gather.9.cloned.1.call-done = bf16[1024,4096]{1,0:T(8,128)(2,1)} async-done(((bf16[128,4096]{1,0:T(8,128)(2,1)}), bf16[1024,4096]{1,0:T(8,128)(2,1)}) %all-gather.9.cloned.1.call-update) | async-done | bytes 8388624 | tf_op jit(solution)/shard_map/all_gather | solution.py:125
  356.2 21.8 %fusion.27 = f32[1024,1792]{1,0:T(8,128)} fusion(bf16[1024,4096]{1,0:T(8,128)(2,1)} %all-gather.9.cloned.1.call-done, bf16[4096,1792]{1,0:T(8,128)(2,1)} %param.17), kind=kOutput, calls=%fused_computation.47 | convolution fusion | flops 15032385536 | bytes 30408704 | tf_op jit(solution)/shard_map/dot_general | solution.py:126
  378.0 23.5 %multiply_convert_fusion = bf16[1024,1792]{1,0:T(8,128)(2,1)} fusion(f32[1024,1792]{1,0:T(8,128)} %fusion.27, bf16[1024,4096]{1,0:T(8,128)(2,1)} %all-gather.9.cloned.1.call-done, bf16[4096,1792]{1,0:T(8,128)(2,1)} %param.18), kind=kOutput, calls=%fused_computation.2 | convolution fusion | flops 15043395584 | bytes 34078720 | tf_op jit(solution)/shard_map/dot_general | solution.py:127
  401.5 19.5 %convolution_convert_fusion = bf16[1024,4096]{1,0:T(8,128)(2,1)} fusion(bf16[1024,1792]{1,0:T(8,128)(2,1)} %multiply_convert_fusion, bf16[1792,4096]{1,0:T(8,128)(2,1)S(1)} %bitcast.55), kind=kOutput, calls=%fused_computation | convolution fusion | flops 15036579840 | bytes 26738688 | tf_op jit(solution)/shard_map/dot_general | solution.py:129
  421.0 52.0 %reduce-scatter.5.cloned.1.call-done = bf16[128,4096]{1,0:T(8,128)(2,1)} async-done(((bf16[1024,4096]{1,0:T(8,128)(2,1)}), bf16[128,4096]{1,0:T(8,128)(2,1)}) %reduce-scatter.5.cloned.1.call-update) | async-done | bytes 1048592 | tf_op jit(solution)/shard_map/reduce_scatter | solution.py:130
  473.1 2.7 fusion.19
  (43 shorter events, 0.8 us)
Async XLA Ops:
  6.5 58.1 %copy-start = (bf16[4096,1,128]{2,0,1:T(8,128)(2,1)S(1)}, bf16[4096,1,128]{2,0,1:T(8,128)(2,1)}, u32[]{:S(2)}) copy-start(bf16[4096,1,128]{2,0,1:T(8,128)(2,1)} %param.13) | copy-start | bytes 3145732
  6.5 58.1 %all-gather.7.cloned.1.call-start = ((), (), s32[]{:S(2)}) async-start(), calls=%async_computation.2 | async-start | bytes 9437184 | tf_op jit(solution)/shard_map/all_gather | solution.py:108
  11.4 111.4 %all-gather.11.cloned.1.call-start = ((), (), s32[]{:S(2)}) async-start(), calls=%async_computation.6 | async-start | bytes 4456448 | tf_op jit(solution)/shard_map/all_gather | solution.py:119
  70.9 1.3 copy-start.8
  71.9 103.9 %all-gather.13.cloned.1.call-start = ((), (), s32[]{:S(2)}) async-start(), calls=%async_computation.7 | async-start | bytes 4456448 | tf_op jit(solution)/shard_map/all_gather | solution.py:120
  78.7 223.1 %reduce-scatter.3.cloned.1.call-start = ((), (), s32[]{:S(2)}) async-start(), calls=%async_computation.3 | async-start | bytes 9437184 | tf_op jit(solution)/shard_map/reduce_scatter | solution.py:123
  92.4 1.2 copy-start.5
  93.6 1.6 copy-start.4
  175.8 67.2 %copy-start.7 = (bf16[4,128,4096]{2,1,0:T(8,128)(2,1)S(1)}, bf16[4,128,4096]{2,1,0:T(8,128)(2,1)}, u32[]{:S(2)}) copy-start(bf16[4,128,4096]{2,1,0:T(8,128)(2,1)} %param.15) | copy-start | bytes 12582916
  249.7 0.7 copy-start.6
  249.7 52.0 %copy-start.2 = (bf16[1,128,4096]{2,1,0:T(8,128)(2,1)S(1)}, bf16[1,128,4096]{2,1,0:T(8,128)(2,1)}, u32[]{:S(2)}) copy-start(bf16[1,128,4096]{2,1,0:T(8,128)(2,1)} %param.10) | copy-start | bytes 3145732
  249.8 106.5 %all-gather.9.cloned.1.call-start = ((), (), s32[]{:S(2)}) async-start(), calls=%async_computation.4 | async-start | bytes 9437184 | tf_op jit(solution)/shard_map/all_gather | solution.py:125
  306.1 167.0 %reduce-scatter.5.cloned.1.call-start = ((), (), s32[]{:S(2)}) async-start(), calls=%async_computation.5 | async-start | bytes 9437184 | tf_op jit(solution)/shard_map/reduce_scatter | solution.py:130
  356.2 45.3 %slice-start = ((s8[14680064]{0:T(1024)(128)(4,1)}), s8[4194304]{0:T(1024)(128)(4,1)S(1)}, s32[]{:S(2)}) async-start(s8[14680064]{0:T(1024)(128)(4,1)} %bitcast.54), calls=%async_computation.8 | async-start | bytes 8388608
  356.2 45.3 %slice-start.1 = ((s8[14680064]{0:T(1024)(128)(4,1)}), s8[4194304]{0:T(1024)(128)(4,1)S(1)}, s32[]{:S(2)}) async-start(s8[14680064]{0:T(1024)(128)(4,1)} %bitcast.54), calls=%async_computation.9 | async-start | bytes 8388608
  378.0 23.5 %slice-start.2 = ((s8[14680064]{0:T(1024)(128)(4,1)}), s8[4194304]{0:T(1024)(128)(4,1)S(1)}, s32[]{:S(2)}) async-start(s8[14680064]{0:T(1024)(128)(4,1)} %bitcast.54), calls=%async_computation.10 | async-start | bytes 8388608
  378.0 23.5 %slice-start.3 = ((s8[14680064]{0:T(1024)(128)(4,1)}), s8[2097152]{0:T(1024)(128)(4,1)S(1)}, s32[]{:S(2)}) async-start(s8[14680064]{0:T(1024)(128)(4,1)} %bitcast.54), calls=%async_computation.11 | async-start | bytes 4194304
  421.0 52.1 %copy-start.3 = (bf16[128,4096]{1,0:T(8,128)(2,1)S(1)}, bf16[128,4096]{1,0:T(8,128)(2,1)}, u32[]{:S(2)}) copy-start(bf16[128,4096]{1,0:T(8,128)(2,1)} %reduce-scatter.3.cloned.1.call-done) | copy-start | bytes 3145732
  421.0 54.7 %copy-start.1 = (bf16[4096,1,128]{2,0,1:T(8,128)(2,1)S(1)}, bf16[4096,1,128]{2,0,1:T(8,128)(2,1)}, u32[]{:S(2)}) copy-start(bf16[4096,1,128]{2,0,1:T(8,128)(2,1)} %param.13) | copy-start | bytes 3145732
Sparse Core Ops, SparseCore 0:
  11.5 53.0 all-gather.6
  72.0 50.8 all-gather.10
  125.0 50.7 all-gather.12
  249.9 51.8 reduce-scatter.2
  306.2 50.0 all-gather.8
  421.1 51.8 reduce-scatter.4

commit v2 on v1

v2 whole, which is shorter than its diff:
```python
import functools
import math
import jax
import jax.numpy as jnp
from jax import lax
from jax.experimental import pallas as pl
from jax.experimental.pallas import tpu as pltpu
from jax.sharding import PartitionSpec as P

NORM_EPS = 1e-5
ROPE_THETA = 500000.0
HD = 128
NX = 4
MESH = pl.DeviceIdType.MESH
F32 = jnp.float32
BF16 = jnp.bfloat16


def params(cid, vmem_mib):
    return pltpu.CompilerParams(collective_id=cid, has_side_effects=True, vmem_limit_bytes=min(vmem_mib * 2 ** 20, 67043328))


def vmem_spec():
    return pl.BlockSpec(memory_space=pltpu.VMEM)


def any_spec():
    return pl.BlockSpec(memory_space=pl.ANY)


def rope_tables(positions):
    inv_freq = ROPE_THETA ** (-2.0 * jnp.arange(HD // 2, dtype=F32) / HD)
    angles = positions.astype(F32)[:, None] * inv_freq[None, :]
    c, s = jnp.cos(angles), jnp.sin(angles)
    return jnp.concatenate([c, c], axis=-1), jnp.concatenate([-s, s], axis=-1)


def enter(peers):
    barrier = pltpu.get_barrier_semaphore()
    for peer in peers:
        pl.semaphore_signal(barrier, inc=1, device_id=peer, device_id_type=MESH)
    pl.semaphore_wait(barrier, len(peers))


def tp_place():
    t = lax.axis_index('tp')
    x, c = t // 2, t % 2
    side = lambda d: {'tp': ((x + d) % NX) * 2 + c}
    return x, c, {'tp': x * 2 + 1 - c}, side(1), side(NX - 1)


GATHER_PARTS = (((0, 0), (0, 1), (1, 0), (1, 1)), ((2, 0), (3, 0), (4, 1), (5, 1)),
                ((2, 1), (3, 1), (4, 0), (5, 0)), ((6, 0), (6, 1), (7, 0), (7, 1)))
GATHER_PLACE = {name: i for i, name in enumerate(n for part in GATHER_PARTS for n in part)}


def norm_into(x_ref, g_ref, full, rows):
    gain = g_ref[...].astype(F32)
    step = min(16, rows)

    @pl.loop(0, rows // step)
    def _(i):
        where = pl.ds(pl.multiple_of(i * step, step), step)
        r = x_ref[where, :].astype(F32)
        mean_sq = jnp.mean(r * r, axis=-1, keepdims=True)
        full[where, :] = (r * lax.rsqrt(mean_sq + NORM_EPS) * gain).astype(BF16)


def gather_and(full, send_sem, recv_sem, half, before, compute):
    x, c, partner, right, left = tp_place()
    started, landing = [], {}

    def send(src, dst, h, device):
        copy = pltpu.make_async_remote_copy(
            src_ref=full.at[pl.ds(GATHER_PLACE[src, h] * half, half)],
            dst_ref=full.at[pl.ds(GATHER_PLACE[dst, h] * half, half)],
            send_sem=send_sem.at[len(started)], recv_sem=recv_sem.at[GATHER_PLACE[dst, h]],
            device_id=device, device_id_type=MESH)
        copy.start()
        started.append(copy)
        landing[dst, h] = copy

    def arrived(*names):
        for name in names:
            landing[name].wait_recv()

    before()
    enter([partner, right, left])
    send(0, 2, 0, right)
    send(0, 4, 1, left)
    send(0, 1, 0, partner)
    send(0, 1, 1, partner)
    send(0, 2, 1, right)
    send(0, 4, 0, left)
    arrived((1, 0), (1, 1))
    compute(0, 0)
    arrived((2, 0))
    send(2, 6, 0, right)
    send(2, 3, 0, partner)
    arrived((4, 1))
    send(4, 6, 1, left)
    send(4, 5, 1, partner)
    compute(0, 1)
    arrived((3, 0), (5, 1))
    compute(1, 0)
    arrived((2, 1))
    send(2, 3, 1, partner)
    arrived((4, 0))
    send(4, 5, 0, partner)
    compute(1, 1)
    arrived((3, 1), (5, 0))
    compute(2, 0)
    arrived((6, 0))
    send(6, 7, 0, partner)
    arrived((6, 1))
    send(6, 7, 1, partner)
    compute(2, 1)
    arrived((7, 0), (7, 1))
    compute(3, 0)
    compute(3, 1)
    for copy in started:
        copy.wait_send()


def part_rows(part, block):
    t = lax.axis_index('tp')
    x, c = t // 2, t % 2
    rows = []
    for name, h in GATHER_PARTS[part]:
        dx, other = (0, 3, 1, 2)[name // 2], name % 2
        core = 1 - c if other else c
        rows.append((((x + dx) % NX) * 2 + core) * block + h * (block // 2))
    return rows


N_SENDS = 14
GATHER_SEMS = [pltpu.SemaphoreType.DMA((N_SENDS,)), pltpu.SemaphoreType.DMA((16,))]


def qkv_kernel(n_heads, x_ref, g_ref, cos_ref, sin_ref, wq_hbm, wk_hbm, wv_hbm, q_ref, kv_ref, full, w, send_sem, recv_sem, w_sem):
    block = x_ref.shape[0]
    half = block // 2
    piece = kv_ref.shape[2]
    width = n_heads * HD
    loads = [pltpu.make_async_copy(wq_hbm, w.at[:, 0:width], w_sem.at[0]),
             pltpu.make_async_copy(wk_hbm, w.at[:, width:width + HD], w_sem.at[1]),
             pltpu.make_async_copy(wv_hbm, w.at[:, width + HD:width + 2 * HD], w_sem.at[2])]

    def before():
        for load in loads:
            load.start()
        norm_into(x_ref, g_ref, full, block)

    def rotate(v, cos, sin):
        f = v.astype(BF16).astype(F32)
        return (f * cos + pltpu.roll(f, HD // 2, 1) * sin).astype(BF16)

    def compute(part, stage):
        rows = [pl.multiple_of(r, half) for r in part_rows(part, block)]
        a = full[part * 4 * half:(part + 1) * 4 * half, :]
        if stage == 0:
            if part == 0:
                for load in loads:
                    load.wait()
            out = jnp.dot(a, w[:, width:width + 2 * HD], preferred_element_type=F32)
            for i, r in enumerate(rows):
                here = slice(i * half, (i + 1) * half)
                where = pl.ds(pl.multiple_of(r % piece, half), half)
                kv_ref[r // piece, 0, where, :] = rotate(out[here, :HD], cos_ref[pl.ds(r, half), :], sin_ref[pl.ds(r, half), :])
                kv_ref[r // piece, 1, where, :] = out[here, HD:].astype(BF16)
            return
        for pair in range(n_heads // 2):
            out = jnp.dot(a, w[:, pair * 2 * HD:(pair + 1) * 2 * HD], preferred_element_type=F32)
            for i, r in enumerate(rows):
                here = slice(i * half, (i + 1) * half)
                cos, sin = cos_ref[pl.ds(r, half), :], sin_ref[pl.ds(r, half), :]
                for k in range(2):
                    q_ref[pl.ds(r, half), (pair * 2 + k) * HD:(pair * 2 + k + 1) * HD] = rotate(out[here, k * HD:(k + 1) * HD], cos, sin)

    gather_and(full, send_sem, recv_sem, half, before, compute)


def gather_qkv(x_rows, g, cos, sin, w_q, w_k, w_v, n_heads, piece):
    block, dim = x_rows.shape
    rows = 2 * NX * block
    width = n_heads * HD
    return pl.pallas_call(
        functools.partial(qkv_kernel, n_heads),
        out_shape=(jax.ShapeDtypeStruct((rows, width), BF16), jax.ShapeDtypeStruct((2, 2, piece, HD), BF16)),
        in_specs=[vmem_spec()] * 4 + [any_spec()] * 3,
        out_specs=(vmem_spec(), vmem_spec()),
        scratch_shapes=[pltpu.VMEM((rows, dim), BF16), pltpu.VMEM((dim, width + 2 * HD), BF16)] + GATHER_SEMS
        + [pltpu.SemaphoreType.DMA((3,))],
        compiler_params=params(0, 48), name='gather_qkv',
        cost_estimate=pl.CostEstimate(flops=2 * rows * dim * (width + 2 * HD), bytes_accessed=2 * dim * (width + 2 * HD), transcendentals=0),
    )(x_rows, g, cos, sin, w_q, w_k, w_v)


def mlp_in_kernel(x_ref, g_ref, wg_hbm, wu_hbm, h_ref, full, wg, wu, send_sem, recv_sem, w_sem):
    block = x_ref.shape[0]
    half = block // 2
    cols = wg.shape[1]
    step = 256
    n_steps = cols // step
    loads = []
    for n in range(n_steps):
        at = slice(n * step, (n + 1) * step)
        loads.append((pltpu.make_async_copy(wg_hbm.at[:, at], wg.at[:, at], w_sem.at[2 * n]),
                      pltpu.make_async_copy(wu_hbm.at[:, at], wu.at[:, at], w_sem.at[2 * n + 1])))

    def before():
        for pair in loads:
            for load in pair:
                load.start()
        norm_into(x_ref, g_ref, full, block)

    def compute(part, stage):
        rows = [pl.multiple_of(r, half) for r in part_rows(part, block)]

        def tile(n, a):
            at = pl.ds(pl.multiple_of(n * step, step), step)
            gate = jnp.dot(a, wg[:, at], preferred_element_type=F32)
            up = jnp.dot(a, wu[:, at], preferred_element_type=F32)
            out = (jax.nn.silu(gate) * up).astype(BF16)
            for i, r in enumerate(rows):
                h_ref[pl.ds(r, half), at] = out[i * half:(i + 1) * half, :]

        split = (n_steps + 1) // 2
        lo, hi = (0, split) if stage == 0 else (split, n_steps)
        if part == 0:
            for n in range(lo, hi):
                for load in loads[n]:
                    load.wait()

        @pl.loop(lo, hi)
        def _(n):
            tile(n, full[part * 4 * half:(part + 1) * 4 * half, :])

    gather_and(full, send_sem, recv_sem, half, before, compute)


def gather_mlp_in(y_rows, g, w_gate, w_up):
    block, dim = y_rows.shape
    rows = 2 * NX * block
    cols = w_gate.shape[1]
    return pl.pallas_call(
        mlp_in_kernel,
        out_shape=jax.ShapeDtypeStruct((rows, cols), BF16),
        in_specs=[vmem_spec()] * 2 + [any_spec()] * 2,
        out_specs=vmem_spec(),
        scratch_shapes=[pltpu.VMEM((rows, dim), BF16), pltpu.VMEM((dim, cols), BF16), pltpu.VMEM((dim, cols), BF16)] + GATHER_SEMS
        + [pltpu.SemaphoreType.DMA((2 * (cols // 256),))],
        compiler_params=params(1, 64), name='gather_mlp_in',
        cost_estimate=pl.CostEstimate(flops=4 * rows * dim * cols, bytes_accessed=4 * dim * cols, transcendentals=rows * cols),
    )(y_rows, g, w_gate, w_up)


def scatter_kernel(h_ref, w_hbm, res_ref, out_ref, w, give, mine, got, passing, last, w_sem, give_sem, got_sem, send_sem, recv_sem):
    x, c, partner, right, left = tp_place()
    block, dim = res_ref.shape
    half = block // 2
    step = 512
    n_steps = dim // step
    loads = []
    for n in range(n_steps):
        at = slice(n * step, (n + 1) * step)
        loads.append(pltpu.make_async_copy(w_hbm.at[:, at], w.at[:, at], w_sem.at[n]))
        loads[-1].start()
    enter([partner, right, left])
    h0, h1 = slice(0, half), slice(half, block)

    def product(dx, core, dst, wait_w=False):
        start = pl.multiple_of((((x + dx) % NX) * 2 + core) * block, block)
        if wait_w:
            for load in loads:
                load.wait()

        @pl.loop(0, n_steps)
        def _(n):
            at = pl.ds(pl.multiple_of(n * step, step), step)
            dst[:, at] = jnp.dot(h_ref[pl.ds(start, block), :], w[:, at], preferred_element_type=F32).astype(BF16)

    def exchange(b, dx, wait_w=False):
        product(dx, 1 - c, give.at[b], wait_w)
        copy = pltpu.make_async_remote_copy(src_ref=give.at[b], dst_ref=got.at[b], send_sem=give_sem.at[b],
                                            recv_sem=got_sem.at[b], device_id=partner, device_id_type=MESH)
        copy.start()
        product(dx, c, mine.at[b])
        return copy

    def add(dst, a, b, rows):
        step_r = min(16, rows)

        @pl.loop(0, rows // step_r)
        def _(i):
            at = pl.ds(pl.multiple_of(i * step_r, step_r), step_r)
            dst[at, :] = (a[at, :].astype(F32) + b[at, :].astype(F32)).astype(BF16)

    started = []

    def send(src, dst, device):
        n = len(started)
        copy = pltpu.make_async_remote_copy(src_ref=src, dst_ref=dst, send_sem=send_sem.at[n], recv_sem=recv_sem.at[n],
                                            device_id=device, device_id_type=MESH)
        copy.start()
        started.append(copy)
        return copy

    pair = exchange(0, 2, True)
    pair.wait_recv()
    add(mine.at[0], mine.at[0], got.at[0], block)
    pass_right = send(mine.at[0, h0], passing.at[0], right)
    pass_left = send(mine.at[0, h1], passing.at[1], left)
    pair_r = exchange(1, 1)
    pair_l = exchange(2, NX - 1)
    pair_r.wait_recv()
    add(mine.at[1], mine.at[1], got.at[1], block)
    to_right_1 = send(mine.at[1, h1], last.at[0, h1], right)
    pair_l.wait_recv()
    add(mine.at[2], mine.at[2], got.at[2], block)
    to_left_0 = send(mine.at[2, h0], last.at[1, h0], left)
    pair_o = exchange(3, 0)
    pass_right.wait_recv()
    add(mine.at[1, h0], mine.at[1, h0], passing.at[0], half)
    to_right_0 = send(mine.at[1, h0], last.at[0, h0], right)
    pass_left.wait_recv()
    add(mine.at[2, h1], mine.at[2, h1], passing.at[1], half)
    to_left_1 = send(mine.at[2, h1], last.at[1, h1], left)
    pair_o.wait_recv()
    for copy in (to_right_1, to_left_0, to_right_0, to_left_1):
        copy.wait_recv()
    step_r = min(16, block)

    @pl.loop(0, block // step_r)
    def _(i):
        at = pl.ds(pl.multiple_of(i * step_r, step_r), step_r)
        total = (mine[3, at, :].astype(F32) + got[3, at, :].astype(F32)) + (last[0, at, :].astype(F32) + last[1, at, :].astype(F32))
        out_ref[at, :] = (res_ref[at, :].astype(F32) + total.astype(BF16).astype(F32)).astype(BF16)

    for copy in (pair, pair_r, pair_l, pair_o, *started):
        copy.wait_send()


def scatter_product(h, w, res, cid):
    rows, depth = h.shape
    block, dim = res.shape
    half = block // 2
    sem = pltpu.SemaphoreType.DMA
    return pl.pallas_call(
        scatter_kernel,
        out_shape=jax.ShapeDtypeStruct((block, dim), BF16),
        in_specs=[vmem_spec(), any_spec(), vmem_spec()],
        out_specs=vmem_spec(),
        scratch_shapes=[pltpu.VMEM((depth, dim), BF16)] + [pltpu.VMEM((4, block, dim), BF16)] * 3
        + [pltpu.VMEM((2, half, dim), BF16), pltpu.VMEM((2, block, dim), BF16),
           sem((max(1, dim // 512),)), sem((4,)), sem((4,)), sem((6,)), sem((6,))],
        compiler_params=params(cid, 48), name='scatter_product_%d' % cid,
        cost_estimate=pl.CostEstimate(flops=2 * rows * dim * depth, bytes_accessed=2 * dim * depth, transcendentals=0),
    )(h, w, res)


def attention_order():
    seq = [((0, 0), 0)]
    waits = {}

    def then(actions, *units):
        waits.setdefault(len(seq), []).extend(actions)
        seq.extend(units)

    first = lambda *s: [(p, 0) for p in s]
    both = lambda *s: [(p, w) for p in s for w in (0, 1)]
    then(['T1'], *first((1, 0), (3, 0)))
    then(['F0'], *first((0, 1), (0, 3)))
    then(['T2'], *first((2, 0)), ((0, 1), 1), ((0, 3), 1))
    then(['F1'], ((1, 0), 1), ((3, 0), 1))
    then(['F3'], *both((1, 1), (1, 3)))
    then(['F2'], *both((3, 1), (3, 3)))
    then(['E0'], ((2, 0), 1), *both((0, 2)))
    then(['E1', 'E3'], *both((1, 2), (3, 2), (2, 1), (2, 3)))
    then(['E2'], *both((2, 2)))
    return seq, waits


def pick(index, values):
    out = index * 0 + values[0]
    for i, v in enumerate(values[1:], 1):
        if v != values[i - 1]:
            out = jnp.where(index >= i, v, out)
    return out


def attention_kernel(n_heads, q_ref, kv_ref, o_ref, m_ref, l_ref, acc_ref, buf, send_sem, recv_sem):
    piece = kv_ref.shape[2]
    me = lax.axis_index('cp')
    y, z = me % NX, me // NX
    scale = HD ** -0.5 * math.log2(math.e)
    at_y = lambda d: {'cp': z * NX + (y + d) % NX}
    at_z = lambda d: {'cp': ((z + d) % NX) * NX + y}
    enter([at_y(1), at_y(3), at_z(1), at_z(3)])
    axes = ((at_y, at_z), (at_z, at_y))

    def slot(kind, da, db):
        dy, dz = (da, db) if kind == 0 else (db, da)
        return dz * NX + dy

    started, landing = [], {}

    def copy_of(kind, src, dst, axis, d, part, n):
        source = kv_ref.at[kind] if src == (0, 0) else buf.at[kind, slot(kind, *src)]
        target = buf.at[kind, slot(kind, *dst)]
        if part is not None:
            source, target = source.at[part], target.at[part]
        return pltpu.make_async_remote_copy(
            src_ref=source, dst_ref=target, send_sem=send_sem.at[n],
            recv_sem=recv_sem.at[kind, slot(kind, *dst), part or 0],
            device_id=axes[kind][axis](d), device_id_type=MESH)

    def send(kind, src, dst, axis, d, part=None):
        key = (kind, src, dst, axis, d, part, len(started))
        copy_of(*key).start()
        started.append(key)
        landing[kind, dst, part] = key

    def landed(*key):
        copy_of(*landing[key]).wait_recv()

    def arrived(kind, *names):
        for name in names:
            for part in ((0, 1) if 2 in name else (None,)):
                landed(kind, name, part)

    def along_b(kind, da):
        send(kind, (da, 0), (da, 3), 1, 1)
        send(kind, (da, 0), (da, 1), 1, 3)

    def act(name):
        step, da = name[0], int(name[1])
        for kind in range(2):
            if name == 'T1':
                arrived(kind, (1, 0), (3, 0))
                send(kind, (3, 0), (2, 0), 0, 1, 0)
                send(kind, (1, 0), (2, 0), 0, 3, 1)
                along_b(kind, 1)
                along_b(kind, 3)
            elif name == 'T2':
                arrived(kind, (2, 0))
                along_b(kind, 2)
            elif step == 'F':
                for db, d, part in ((3, 1, 0), (1, 3, 1)):
                    if da == 2:
                        landed(kind, (2, db), None)
                    else:
                        arrived(kind, (da, db))
                    send(kind, (da, db), (da, 2), 1, d, part)
            else:
                for part in (0, 1):
                    landed(kind, (da, 2), part)

    kinds = (0, 1)
    for kind in kinds:
        send(kind, (0, 0), (3, 0), 0, 1)
        send(kind, (0, 0), (1, 0), 0, 3)
    for kind in kinds:
        along_b(kind, 0)

    m_ref[...] = jnp.full_like(m_ref, -1e30)
    l_ref[...] = jnp.zeros_like(l_ref)
    acc_ref[...] = jnp.zeros_like(acc_ref)

    def unit(q_row, k, v, masked):
        rows = pl.ds(pl.multiple_of(q_row, piece), piece)
        for h in range(n_heads):
            cols = slice(h * HD, (h + 1) * HD)
            s = lax.dot_general(q_ref[rows, cols], k, (((1,), (1,)), ((), ())), preferred_element_type=F32) * scale
            if masked:
                row = lax.broadcasted_iota(jnp.int32, (piece, piece), 0)
                col = lax.broadcasted_iota(jnp.int32, (piece, piece), 1)
                s = jnp.where(row >= col, s, -1e30)
            m_old = m_ref[rows, cols]
            m_new = jnp.maximum(m_old, jnp.max(s, axis=1, keepdims=True))
            alpha = jnp.exp2(m_old - m_new)
            p = [jnp.exp2(s[:, i * HD:(i + 1) * HD] - m_new) for i in range(piece // HD)]
            psum = p[0]
            for part in p[1:]:
                psum = psum + part
            l_ref[rows, cols] = l_ref[rows, cols] * alpha + psum
            pb = jnp.concatenate([part.astype(BF16) for part in p], axis=1)
            pv = jnp.dot(pb, v, preferred_element_type=F32)
            acc_ref[rows, cols] = acc_ref[rows, cols] * alpha + pv
            m_ref[rows, cols] = m_new

    @pl.loop(0, 2)
    def _(kind):
        unit(kind * piece, kv_ref[kind, 0], kv_ref[kind, 1], True)

    unit(piece, kv_ref[0, 0], kv_ref[0, 1], False)
    seq, waits = attention_order()
    marks = sorted(waits) + [len(seq)]

    @pl.loop(1, len(seq))
    def _(u):
        for mark in marks[:-1]:
            @pl.when(u == mark)
            def _():
                for name in waits[mark]:
                    act(name)

        dy = pick(u, [p[0] for p, _ in seq])
        dz = pick(u, [p[1] for p, _ in seq])
        which = pick(u, [w for _, w in seq])
        src = ((z + dz) % NX) * NX + (y + dy) % NX
        late = jnp.where(src > me, 1, 0)
        q_row = jnp.where(which == 0, 1, late) * piece
        kind = which * late
        at = dz * NX + dy
        unit(q_row, buf[kind, at, 0], buf[kind, at, 1], False)

    @pl.loop(0, 2)
    def _(part):
        rows = pl.ds(pl.multiple_of(part * piece, piece), piece)
        for h in range(n_heads):
            cols = slice(h * HD, (h + 1) * HD)
            total = jnp.sum(l_ref[rows, cols], axis=1, keepdims=True)
            o_ref[rows, cols] = (acc_ref[rows, cols] / total).astype(BF16)

    for key in started:
        copy_of(*key).wait_send()


def attention(q, kv):
    rows, width = q.shape
    piece = kv.shape[2]
    sem = pltpu.SemaphoreType.DMA
    return pl.pallas_call(
        functools.partial(attention_kernel, width // HD),
        out_shape=jax.ShapeDtypeStruct((rows, width), BF16),
        in_specs=[vmem_spec()] * 2,
        out_specs=vmem_spec(),
        scratch_shapes=[pltpu.VMEM((rows, width), F32)] * 3 + [pltpu.VMEM((2, NX * NX, 2, piece, HD), BF16),
                                                              sem((40,)), sem((2, NX * NX, 2))],
        compiler_params=params(2, 48), name='attention',
        cost_estimate=pl.CostEstimate(flops=18 * 10 ** 9, bytes_accessed=10 * 2 ** 20, transcendentals=35 * 10 ** 6),
    )(q, kv)


def solution(mesh):
    row_spec = P('dp', ('cp', 'tp'), None)
    head_cols = P(None, 'tp', None)
    cp_size = mesh.shape['cp']

    def local_layer(x, g_attn, w_q, w_k, w_v, w_o, g_mlp, w_gate, w_up, w_down):
        x_rows = x[0]
        block, dim = x_rows.shape
        rows = block * mesh.shape['tp']
        piece = rows // 2
        cp_index = lax.axis_index('cp')
        n_heads = w_q.shape[1]
        j = jnp.arange(rows, dtype=jnp.int32)
        positions = jnp.where(j < piece, cp_index * piece + j, (2 * cp_size - 1 - cp_index) * piece + j - piece)
        cos, sin = rope_tables(positions)
        q, kv = gather_qkv(x_rows, g_attn.reshape(1, dim), cos, sin, w_q.reshape(dim, n_heads * HD),
                           w_k.reshape(dim, HD), w_v.reshape(dim, HD), n_heads, piece)
        o = attention(q, kv)
        y_rows = scatter_product(o, w_o.reshape(n_heads * HD, dim), x_rows, 3)
        hidden = gather_mlp_in(y_rows, g_mlp.reshape(1, dim), w_gate, w_up)
        z_rows = scatter_product(hidden, w_down, y_rows, 4)
        return z_rows[None]

    return jax.shard_map(local_layer, mesh=mesh,
                         in_specs=(row_spec, P(), head_cols, head_cols, head_cols, P('tp', None, None),
                                   P(), P(None, 'tp'), P(None, 'tp'), P('tp', None)),
                         out_specs=row_spec, check_vma=False)
```

time: 488 us -> 294 us (0.60)
  waiting for transfers between devices: 279 us -> 0 us
  Pallas kernels: 67.2 us -> 283 us
  matrix products: 94.5 us -> 0 us
  between operations: 14.1 us -> 0.15 us
  other arithmetic: 15.7 us -> 2.26 us
    pallas_call x1 -> x5, Pallas kernels: 67.2 us -> 283 us  [the longest x2 94.5 us: scatter_product(): pl.pallas_call(scatter_kernel, out_shape=jax.ShapeDtypeStruct((block, dim...]
    all_gather x4 -> x0, waiting for transfers between devices: 175 us -> none  [the longest x1 52.1 us: local_layer(): normed = lax.all_gather(rms_norm(x_rows, g_attn), 'tp', axis=0, tiled=True)]
    reduce_scatter x2 -> x0, waiting for transfers between devices: 103 us -> none  [the longest x1 52 us: local_layer(): lax.psum_scatter(down_part, 'tp', scatter_dimension=0, tiled=True)]
    dot_general x7 -> x0, matrix products: 94.5 us -> none  [the longest x1 23.5 us: local_layer(): up_proj = jnp.dot(normed_mlp, w_up, preferred_element_type=jnp.float32)]
    convert_element_type x7 -> x1, other arithmetic: 7.56 us -> 0.01 us  [rope_tables(): angles = positions.astype(F32)[:, None] * inv_freq[None, :]]
    unnamed x26 -> x20, local copies, waits for them, and re-layouts: 0.99 us -> 7.91 us
    all_gather x1 -> x0, local copies, waits for them, and re-layouts: 6.36 us -> none  [local_layer(): k_seq = lax.all_gather(k, 'cp', axis=0, tiled=False)]
  transfers between devices with their start and end apart: 6 -> 0, of which waited for: 6 -> 0; matrix products, arithmetic and copies ran while one was open for 6% -> 0% of each run, Pallas kernels for 0% -> 0%
where the time goes in v2:
time: 294 us; the launch traced here: 293 us
  Pallas kernels  283 us (96%)
  local copies, waits for them, and re-layouts  8.53 us (3%)
    pallas_call x2, Pallas kernels, scatter_product(): pl.pallas_call(scatter_kernel, out_shape=jax.ShapeDtypeStruct((block, dim...  94.5 us
    pallas_call x1, Pallas kernels, attention(): pl.pallas_call(functools.partial(attention_kernel, width // HD), out_shap...  87.8 us
    pallas_call x1, Pallas kernels, gather_mlp_in(): pl.pallas_call(mlp_in_kernel, out_shape=jax.ShapeDtypeStruct((rows, cols)...  54.3 us
    pallas_call x1, Pallas kernels, gather_qkv(): pl.pallas_call(functools.partial(qkv_kernel, n_heads), out_shape=(jax.Sha...  45.9 us
    unnamed x20, local copies, waits for them, and re-layouts  7.91 us

profile of v2, /device:TPU:1, one launch (start us, length us, event | category | flops | bytes accessed | tf_op | source)
XLA Modules:
  0.0 293.5 jit_solution(1538255284488858190)
XLA Ops:
  0.0 0.0 copy-start.6
  0.0 1.9 fusion
  1.9 0.3 pad_maximum_fusion
  2.3 0.0 copy-done.6
  2.3 0.0 copy-start.7
  2.3 0.0 copy-start
  2.3 0.0 copy-start.1
  2.3 0.0 copy-start.2
  2.3 2.7 copy.13
  5.0 0.0 copy-done.7
  5.0 0.0 copy-done
  5.0 0.0 copy-done.1
  5.1 0.0 copy-done.2
  5.1 45.9 %gather_qkv.1 = (bf16[1024,512]{1,0:T(8,128)(2,1)S(1)}, bf16[2,2,512,128]{3,2,1,0:T(8,128)(2,1)S(1)}) custom-call(bf16[128,4096]{1,0:T(8,128)(2,1)S(1)} %bitcast.12, bf16[1,4096]{1,0:T(2,128)(2,1)S(1)} %reshape.34.g_ref, f32[1024,128]{1,0:T(8,128)S(1)} %get-tuple-element.12.cos_ref, f32[1024,128]{1,0:T(8,128)S(1)} %get-tuple-element.13.sin_ref, ...), custom_call_target="tpu_custom_call" | custom-call | flops 6442450944 | bytes 6291456 | tf_op jit(solution)/shard_map/gather_qkv/pallas_call | solution.py:187
  51.0 87.8 %attention.1.h_ref = bf16[1024,512]{1,0:T(8,128)(2,1)S(1)} custom-call(bf16[1024,512]{1,0:T(8,128)(2,1)S(1)} %get-tuple-element.7.q_ref, bf16[2,2,512,128]{3,2,1,0:T(8,128)(2,1)S(1)} %get-tuple-element.8.kv_ref), custom_call_target="tpu_custom_call" | custom-call | flops 17999998976 | bytes 10485760 | tf_op jit(solution)/shard_map/attention/pallas_call | solution.py:534
  138.8 0.0 copy-start.8
  138.8 44.4 %scatter_product_3.1.x_ref.res_ref = bf16[128,4096]{1,0:T(8,128)(2,1)S(1)} custom-call(bf16[1024,512]{1,0:T(8,128)(2,1)S(1)} %attention.1.h_ref, bf16[512,4096]{1,0:T(8,128)(2,1)} %bitcast.16, bf16[128,4096]{1,0:T(8,128)(2,1)S(1)} %bitcast.13), custom_call_target="tpu_custom_call" | custom-call | flops 4294967296 | bytes 4194304 | tf_op jit(solution)/shard_map/scatter_product_3/pallas_call | solution.py:349
  183.3 0.0 copy-start.3
  183.3 1.0 copy-done.3
  184.2 0.0 copy-done.8
  184.2 0.6 reshape.39.g_ref
  184.8 54.3 %gather_mlp_in.1.h_ref = bf16[1024,1792]{1,0:T(8,128)(2,1)} custom-call(bf16[128,4096]{1,0:T(8,128)(2,1)} %copy-done.3, bf16[1,4096]{1,0:T(2,128)(2,1)} %reshape.39.g_ref, bf16[4096,1792]{1,0:T(8,128)(2,1)} %wg_hbm.1, bf16[4096,1792]{1,0:T(8,128)(2,1)} %wu_hbm.1), custom_call_target="tpu_custom_call" | custom-call | flops 30064771072 | bytes 29360128 | tf_op jit(solution)/shard_map/gather_mlp_in/pallas_call | solution.py:246
  239.1 0.0 copy-start.4
  239.1 1.2 copy-done.4
  240.4 0.0 copy-start.5
  240.4 2.0 copy-done.5
  242.4 50.1 %scatter_product_4.1 = bf16[128,4096]{1,0:T(8,128)(2,1)S(1)} custom-call(bf16[1024,1792]{1,0:T(8,128)(2,1)S(1)} %copy-done.5, bf16[1792,4096]{1,0:T(8,128)(2,1)} %w_hbm.1, bf16[128,4096]{1,0:T(8,128)(2,1)S(1)} %copy-done.4), custom_call_target="tpu_custom_call" | custom-call | flops 15032385536 | bytes 14680064 | tf_op jit(solution)/shard_map/scatter_product_4/pallas_call | solution.py:349
  292.5 1.0 copy.15
  (3 shorter events, 0.0 us)
Async XLA Ops:
  0.0 2.3 copy-start.6
  2.3 2.7 copy-start.7
  2.3 2.7 copy-start
  2.3 2.7 copy-start.1
  2.3 2.7 copy-start.2
  138.8 45.4 %copy-start.8 = (bf16[4096]{0:T(1024)(128)(2,1)S(1)}, bf16[4096]{0:T(1024)(128)(2,1)}, u32[]{:S(2)}) copy-start(bf16[4096]{0:T(1024)(128)(2,1)} %param.16) | copy-start | bytes 24580
  183.3 1.0 copy-start.3
  239.1 1.2 copy-start.4
  240.4 2.0 copy-start.5

commit v3 on v2

--- a/solution.py
+++ b/solution.py
@@ -49,9 +49,15 @@
     return x, c, {'tp': x * 2 + 1 - c}, side(1), side(NX - 1)
 
 
-GATHER_PARTS = (((0, 0), (0, 1), (1, 0), (1, 1)), ((2, 0), (3, 0), (4, 1), (5, 1)),
-                ((2, 1), (3, 1), (4, 0), (5, 0)), ((6, 0), (6, 1), (7, 0), (7, 1)))
+OWN, MATE, LEFT, LEFT_MATE, RIGHT, RIGHT_MATE, FAR, FAR_MATE = range(8)
+LO, HI = range(2)
+NEAR_PART, FIRST_PART, LAST_PART, FAR_PART = range(4)
+GATHER_PARTS = (((OWN, LO), (OWN, HI), (MATE, LO), (MATE, HI)),
+                ((LEFT, LO), (RIGHT, HI), (LEFT_MATE, LO), (RIGHT_MATE, HI)),
+                ((LEFT, HI), (RIGHT, LO), (LEFT_MATE, HI), (RIGHT_MATE, LO)),
+                ((FAR, LO), (FAR, HI), (FAR_MATE, LO), (FAR_MATE, HI)))
 GATHER_PLACE = {name: i for i, name in enumerate(n for part in GATHER_PARTS for n in part)}
+N_PLACES = len(GATHER_PLACE)
 
 
 def norm_into(x_ref, g_ref, full, rows):
@@ -66,60 +72,59 @@
         full[where, :] = (r * lax.rsqrt(mean_sq + NORM_EPS) * gain).astype(BF16)
 
 
-def gather_and(full, send_sem, recv_sem, half, before, compute):
-    x, c, partner, right, left = tp_place()
-    started, landing = [], {}
-
-    def send(src, dst, h, device):
+class Gather:
+    def __init__(self, full, send_sem, recv_sem, half):
+        self.full, self.send_sem, self.recv_sem, self.half = full, send_sem, recv_sem, half
+        _, _, self.mate, self.right, self.left = tp_place()
+        self.started, self.landing = [], {}
+
+    def enter(self):
+        enter([self.mate, self.right, self.left])
+
+    def send(self, src, dst, h, device):
+        rows = [pl.ds(GATHER_PLACE[slot, h] * self.half, self.half) for slot in (src, dst)]
         copy = pltpu.make_async_remote_copy(
-            src_ref=full.at[pl.ds(GATHER_PLACE[src, h] * half, half)],
-            dst_ref=full.at[pl.ds(GATHER_PLACE[dst, h] * half, half)],
-            send_sem=send_sem.at[len(started)], recv_sem=recv_sem.at[GATHER_PLACE[dst, h]],
+            src_ref=self.full.at[rows[0]], dst_ref=self.full.at[rows[1]],
+            send_sem=self.send_sem.at[len(self.started)], recv_sem=self.recv_sem.at[GATHER_PLACE[dst, h]],
             device_id=device, device_id_type=MESH)
         copy.start()
-        started.append(copy)
-        landing[dst, h] = copy
-
-    def arrived(*names):
+        self.started.append(copy)
+        self.landing[dst, h] = copy
+
+    def arrived(self, *names):
         for name in names:
-            landing[name].wait_recv()
-
-    before()
-    enter([partner, right, left])
-    send(0, 2, 0, right)
-    send(0, 4, 1, left)
-    send(0, 1, 0, partner)
-    send(0, 1, 1, partner)
-    send(0, 2, 1, right)
-    send(0, 4, 0, left)
-    arrived((1, 0), (1, 1))
-    compute(0, 0)
-    arrived((2, 0))
-    send(2, 6, 0, right)
-    send(2, 3, 0, partner)
-    arrived((4, 1))
-    send(4, 6, 1, left)
-    send(4, 5, 1, partner)
-    compute(0, 1)
-    arrived((3, 0), (5, 1))
-    compute(1, 0)
-    arrived((2, 1))
-    send(2, 3, 1, partner)
-    arrived((4, 0))
-    send(4, 5, 0, partner)
-    compute(1, 1)
-    arrived((3, 1), (5, 0))
-    compute(2, 0)
-    arrived((6, 0))
-    send(6, 7, 0, partner)
-    arrived((6, 1))
-    send(6, 7, 1, partner)
-    compute(2, 1)
-    arrived((7, 0), (7, 1))
-    compute(3, 0)
-    compute(3, 1)
-    for copy in started:
-        copy.wait_send()
+            self.landing[name].wait_recv()
+
+    def start(self):
+        self.send(OWN, LEFT, LO, self.right)
+        self.send(OWN, RIGHT, HI, self.left)
+        for h in (LO, HI):
+            self.send(OWN, MATE, h, self.mate)
+
+    def relay(self):
+        self.arrived((LEFT, LO))
+        self.send(LEFT, FAR, LO, self.right)
+        self.send(OWN, LEFT, HI, self.right)
+        self.arrived((RIGHT, HI))
+        self.send(RIGHT, FAR, HI, self.left)
+        self.send(OWN, RIGHT, LO, self.left)
+        self.send(LEFT, LEFT_MATE, LO, self.mate)
+        self.send(RIGHT, RIGHT_MATE, HI, self.mate)
+
+    def share_far(self):
+        for h in (LO, HI):
+            self.arrived((FAR, h))
+            self.send(FAR, FAR_MATE, h, self.mate)
+
+    def share_last(self):
+        self.arrived((LEFT, HI))
+        self.send(LEFT, LEFT_MATE, HI, self.mate)
+        self.arrived((RIGHT, LO))
+        self.send(RIGHT, RIGHT_MATE, LO, self.mate)
+
+    def sent(self, *which):
+        for copy in self.started:
+            copy.wait_send()
 
 
 def part_rows(part, block):
@@ -127,14 +132,14 @@
     x, c = t // 2, t % 2
     rows = []
     for name, h in GATHER_PARTS[part]:
-        dx, other = (0, 3, 1, 2)[name // 2], name % 2
+        dx, other = {OWN: 0, LEFT: NX - 1, RIGHT: 1, FAR: 2}[name // 2 * 2], name % 2
         core = 1 - c if other else c
         rows.append((((x + dx) % NX) * 2 + core) * block + h * (block // 2))
     return rows
 
 
 N_SENDS = 14
-GATHER_SEMS = [pltpu.SemaphoreType.DMA((N_SENDS,)), pltpu.SemaphoreType.DMA((16,))]
+GATHER_SEMS = [pltpu.SemaphoreType.DMA((N_SENDS,)), pltpu.SemaphoreType.DMA((N_PLACES,))]
 
 
 def qkv_kernel(n_heads, x_ref, g_ref, cos_ref, sin_ref, wq_hbm, wk_hbm, wv_hbm, q_ref, kv_ref, full, w, send_sem, recv_sem, w_sem):
@@ -146,38 +151,54 @@
              pltpu.make_async_copy(wk_hbm, w.at[:, width:width + HD], w_sem.at[1]),
              pltpu.make_async_copy(wv_hbm, w.at[:, width + HD:width + 2 * HD], w_sem.at[2])]
 
-    def before():
-        for load in loads:
-            load.start()
-        norm_into(x_ref, g_ref, full, block)
-
     def rotate(v, cos, sin):
         f = v.astype(BF16).astype(F32)
         return (f * cos + pltpu.roll(f, HD // 2, 1) * sin).astype(BF16)
 
-    def compute(part, stage):
-        rows = [pl.multiple_of(r, half) for r in part_rows(part, block)]
-        a = full[part * 4 * half:(part + 1) * 4 * half, :]
-        if stage == 0:
-            if part == 0:
-                for load in loads:
-                    load.wait()
-            out = jnp.dot(a, w[:, width:width + 2 * HD], preferred_element_type=F32)
-            for i, r in enumerate(rows):
-                here = slice(i * half, (i + 1) * half)
-                where = pl.ds(pl.multiple_of(r % piece, half), half)
-                kv_ref[r // piece, 0, where, :] = rotate(out[here, :HD], cos_ref[pl.ds(r, half), :], sin_ref[pl.ds(r, half), :])
-                kv_ref[r // piece, 1, where, :] = out[here, HD:].astype(BF16)
-            return
-        for pair in range(n_heads // 2):
-            out = jnp.dot(a, w[:, pair * 2 * HD:(pair + 1) * 2 * HD], preferred_element_type=F32)
+    def keys_values(part, rows, a):
+        out = jnp.dot(a, w[:, width:], preferred_element_type=F32)
+        for i, r in enumerate(rows):
+            here = slice(i * half, (i + 1) * half)
+            where = pl.ds(pl.multiple_of(r % piece, half), half)
+            kv_ref[r // piece, 0, where, :] = rotate(out[here, :HD], cos_ref[pl.ds(r, half), :], sin_ref[pl.ds(r, half), :])
+            kv_ref[r // piece, 1, where, :] = out[here, HD:].astype(BF16)
+
+    def queries(part, rows, a):
+        for start in range(0, width, 2 * HD):
+            out = jnp.dot(a, w[:, start:start + 2 * HD], preferred_element_type=F32)
             for i, r in enumerate(rows):
                 here = slice(i * half, (i + 1) * half)
                 cos, sin = cos_ref[pl.ds(r, half), :], sin_ref[pl.ds(r, half), :]
-                for k in range(2):
-                    q_ref[pl.ds(r, half), (pair * 2 + k) * HD:(pair * 2 + k + 1) * HD] = rotate(out[here, k * HD:(k + 1) * HD], cos, sin)
-
-    gather_and(full, send_sem, recv_sem, half, before, compute)
+                for k in (0, HD):
+                    q_ref[pl.ds(r, half), start + k:start + k + HD] = rotate(out[here, k:k + HD], cos, sin)
+
+    def compute(part):
+        rows = [pl.multiple_of(r, half) for r in part_rows(part, block)]
+        n = len(rows) * half
+        a = full[part * n:(part + 1) * n, :]
+        keys_values(part, rows, a)
+        queries(part, rows, a)
+
+    gather = Gather(full, send_sem, recv_sem, half)
+    for load in loads:
+        load.start()
+    norm_into(x_ref, g_ref, full, block)
+    gather.enter()
+    gather.start()
+    gather.arrived((MATE, LO), (MATE, HI))
+    for load in loads:
+        load.wait()
+    compute(NEAR_PART)
+    gather.relay()
+    gather.arrived((LEFT_MATE, LO), (RIGHT_MATE, HI))
+    compute(FIRST_PART)
+    gather.share_far()
+    gather.arrived((FAR_MATE, LO), (FAR_MATE, HI))
+    compute(FAR_PART)
+    gather.share_last()
+    gather.arrived((LEFT_MATE, HI), (RIGHT_MATE, LO))
+    compute(LAST_PART)
+    gather.sent()
 
 
 def gather_qkv(x_rows, g, cos, sin, w_q, w_k, w_v, n_heads, piece):
@@ -196,8 +217,30 @@
     )(x_rows, g, cos, sin, w_q, w_k, w_v)
 
 
-def mlp_in_kernel(x_ref, g_ref, wg_hbm, wu_hbm, h_ref, full, wg, wu, send_sem, recv_sem, w_sem):
-    block = x_ref.shape[0]
+def add_rows(dst, a, b):
+    step = min(16, dst.shape[0])
+
+    @pl.loop(0, dst.shape[0] // step)
+    def _(i):
+        at = pl.ds(pl.multiple_of(i * step, step), step)
+        dst[at, :] = (a[at, :].astype(F32) + b[at, :].astype(F32)).astype(BF16)
+
+
+def finish_rows(out, res, parts):
+    step = min(16, out.shape[0])
+
+    @pl.loop(0, out.shape[0] // step)
+    def _(i):
+        at = pl.ds(pl.multiple_of(i * step, step), step)
+        total = parts[0][at, :].astype(F32)
+        for part in parts[1:]:
+            total = total + part[at, :].astype(F32)
+        out[at, :] = (res[at, :].astype(F32) + total.astype(BF16).astype(F32)).astype(BF16)
+
+
+def mlp_kernel(y_hbm, g_ref, wg_hbm, wu_hbm, wd_hbm, z_hbm, full, wg, wu, wd, hid, give, got, passing, last,
+               send_sem, recv_sem, w_sem, d_sem, mate_sems, row_sems, io_sem):
+    block, dim = y_hbm.shape
     half = block // 2
     cols = wg.shape[1]
     step = 256
@@ -205,54 +248,140 @@
     loads = []
     for n in range(n_steps):
         at = slice(n * step, (n + 1) * step)
-        loads.append((pltpu.make_async_copy(wg_hbm.at[:, at], wg.at[:, at], w_sem.at[2 * n]),
-                      pltpu.make_async_copy(wu_hbm.at[:, at], wu.at[:, at], w_sem.at[2 * n + 1])))
-
-    def before():
-        for pair in loads:
-            for load in pair:
-                load.start()
-        norm_into(x_ref, g_ref, full, block)
-
-    def compute(part, stage):
-        rows = [pl.multiple_of(r, half) for r in part_rows(part, block)]
-
-        def tile(n, a):
+        loads.append((pltpu.make_async_copy(wg_hbm.at[:, at], wg.at[:, at], w_sem.at[0, n]),
+                      pltpu.make_async_copy(wu_hbm.at[:, at], wu.at[:, at], w_sem.at[1, n])))
+    load_d = pltpu.make_async_copy(wd_hbm, wd, d_sem)
+    gather = Gather(full, send_sem, recv_sem, half)
+    n_rows = 2 * block
+    head, tail = slice(0, half), slice(half, block)
+
+    def gate_up(part, lo, hi):
+        @pl.loop(lo, hi)
+        def _(n):
             at = pl.ds(pl.multiple_of(n * step, step), step)
+            a = full[part * n_rows:(part + 1) * n_rows, :]
             gate = jnp.dot(a, wg[:, at], preferred_element_type=F32)
             up = jnp.dot(a, wu[:, at], preferred_element_type=F32)
-            out = (jax.nn.silu(gate) * up).astype(BF16)
-            for i, r in enumerate(rows):
-                h_ref[pl.ds(r, half), at] = out[i * half:(i + 1) * half, :]
-
-        split = (n_steps + 1) // 2
-        lo, hi = (0, split) if stage == 0 else (split, n_steps)
-        if part == 0:
-            for n in range(lo, hi):
-                for load in loads[n]:
-                    load.wait()
-
-        @pl.loop(lo, hi)
+            hid[part, :, at] = (jax.nn.silu(gate) * up).astype(BF16)
+
+    def down(part, mine, dst):
+        wide = min(512, dim)
+
+        @pl.loop(0, dim // wide)
         def _(n):
-            tile(n, full[part * 4 * half:(part + 1) * 4 * half, :])
-
-    gather_and(full, send_sem, recv_sem, half, before, compute)
-
-
-def gather_mlp_in(y_rows, g, w_gate, w_up):
+            at = pl.ds(pl.multiple_of(n * wide, wide), wide)
+            a = hid[part, 0:block, :] if mine else hid[part, block:n_rows, :]
+            dst[:, at] = jnp.dot(a, wd[:, at], preferred_element_type=F32).astype(BF16)
+
+    kept = {FAR_PART: full.at[block:n_rows], FIRST_PART: full.at[2 * n_rows - block:2 * n_rows],
+            LAST_PART: full.at[n_rows:n_rows + block], NEAR_PART: full.at[0:block]}
+    traded, moved = {}, []
+
+    def trade(part, buffer):
+        down(part, False, give.at[buffer])
+        traded[part] = pltpu.make_async_remote_copy(
+            src_ref=give.at[buffer], dst_ref=got.at[part], send_sem=mate_sems.at[0, part], recv_sem=mate_sems.at[1, part],
+            device_id=gather.mate, device_id_type=MESH)
+        traded[part].start()
+
+    def join(part):
+        traded[part].wait_recv()
+        add_rows(kept[part], kept[part], got.at[part])
+
+    def move(src, dst, device):
+        copy = pltpu.make_async_remote_copy(src_ref=src, dst_ref=dst, send_sem=row_sems.at[0, len(moved)],
+                                            recv_sem=row_sems.at[1, len(moved)], device_id=device, device_id_type=MESH)
+        copy.start()
+        moved.append(copy)
+        return copy
+
+    fetch = pltpu.make_async_copy(y_hbm, give.at[0], io_sem)
+    fetch.start()
+    for pair in loads:
+        for load in pair:
+            load.start()
+    load_d.start()
+    fetch.wait()
+    norm_into(give.at[0], g_ref, full, block)
+    gather.enter()
+    gather.start()
+    gather.arrived((MATE, LO), (MATE, HI))
+    split = (n_steps + 1) // 2
+    for lo, hi in ((0, split), (split, n_steps)):
+        for pair in loads[lo:hi]:
+            for load in pair:
+                load.wait()
+        gate_up(NEAR_PART, lo, hi)
+        if lo == 0:
+            gather.relay()
+    gather.arrived((LEFT_MATE, LO), (RIGHT_MATE, HI))
+    gate_up(FIRST_PART, 0, n_steps - 1)
+    gather.share_far()
+    gate_up(FIRST_PART, n_steps - 1, n_steps)
+    gather.arrived((FAR_MATE, LO), (FAR_MATE, HI))
+    gate_up(FAR_PART, 0, n_steps)
+    load_d.wait()
+    trade(FAR_PART, 0)
+    down(FAR_PART, True, kept[FAR_PART])
+    gather.share_last()
+    join(FAR_PART)
+    pass_right = move(kept[FAR_PART].at[head], passing.at[0], gather.right)
+    pass_left = move(kept[FAR_PART].at[tail], passing.at[1], gather.left)
+    gather.arrived((LEFT_MATE, HI), (RIGHT_MATE, LO))
+    gather.sent()
+    trade(FIRST_PART, 1)
+    down(FIRST_PART, True, kept[FIRST_PART])
+    gate_up(LAST_PART, 0, split)
+    join(FIRST_PART)
+    moved_first = [move(kept[FIRST_PART].at[head], last.at[1, head], gather.left),
+                   move(kept[FIRST_PART].at[tail], last.at[0, tail], gather.right)]
+    gate_up(LAST_PART, split, n_steps)
+    traded[FAR_PART].wait_send()
+    trade(LAST_PART, 0)
+    down(LAST_PART, True, kept[LAST_PART])
+    traded[FIRST_PART].wait_send()
+    trade(NEAR_PART, 1)
+    join(LAST_PART)
+    pass_left.wait_recv()
+    add_rows(kept[LAST_PART].at[head], kept[LAST_PART].at[head], passing.at[1])
+    pass_right.wait_recv()
+    add_rows(kept[LAST_PART].at[tail], kept[LAST_PART].at[tail], passing.at[0])
+    moved_last = [move(kept[LAST_PART].at[head], last.at[1, tail], gather.left),
+                  move(kept[LAST_PART].at[tail], last.at[0, head], gather.right)]
+    down(NEAR_PART, True, kept[NEAR_PART])
+    traded[LAST_PART].wait_send()
+    fetch.start()
+    traded[NEAR_PART].wait_recv()
+    fetch.wait()
+    for copy in moved_first + moved_last:
+        copy.wait_recv()
+    done = full.at[3 * n_rows:3 * n_rows + block]
+    finish_rows(done, give.at[0], [kept[NEAR_PART], got.at[NEAR_PART], last.at[0], last.at[1]])
+    put = pltpu.make_async_copy(done, z_hbm, io_sem)
+    put.start()
+    traded[NEAR_PART].wait_send()
+    for copy in moved:
+        copy.wait_send()
+    put.wait()
+
+
+def mlp(y_rows, g, w_gate, w_up, w_down):
     block, dim = y_rows.shape
     rows = 2 * NX * block
     cols = w_gate.shape[1]
+    sem = pltpu.SemaphoreType.DMA
+    buffer = lambda *shape: pltpu.VMEM(shape, BF16)
     return pl.pallas_call(
-        mlp_in_kernel,
-        out_shape=jax.ShapeDtypeStruct((rows, cols), BF16),
-        in_specs=[vmem_spec()] * 2 + [any_spec()] * 2,
-        out_specs=vmem_spec(),
-        scratch_shapes=[pltpu.VMEM((rows, dim), BF16), pltpu.VMEM((dim, cols), BF16), pltpu.VMEM((dim, cols), BF16)] + GATHER_SEMS
-        + [pltpu.SemaphoreType.DMA((2 * (cols // 256),))],
-        compiler_params=params(1, 64), name='gather_mlp_in',
-        cost_estimate=pl.CostEstimate(flops=4 * rows * dim * cols, bytes_accessed=4 * dim * cols, transcendentals=rows * cols),
-    )(y_rows, g, w_gate, w_up)
+        mlp_kernel,
+        out_shape=jax.ShapeDtypeStruct((block, dim), BF16),
+        in_specs=[any_spec(), vmem_spec()] + [any_spec()] * 3,
+        out_specs=any_spec(),
+        scratch_shapes=[buffer(rows, dim), buffer(dim, cols), buffer(dim, cols), buffer(cols, dim), buffer(NX, 2 * block, cols),
+                        buffer(2, block, dim), buffer(NX, block, dim), buffer(2, block // 2, dim), buffer(2, block, dim)]
+        + GATHER_SEMS + [sem((2, cols // 256)), sem, sem((2, NX)), sem((2, 6)), sem],
+        compiler_params=params(1, 64), name='mlp',
+        cost_estimate=pl.CostEstimate(flops=6 * rows * dim * cols, bytes_accessed=6 * dim * cols, transcendentals=rows * cols),
+    )(y_rows, g, w_gate, w_up, w_down)
 
 
 def scatter_kernel(h_ref, w_hbm, res_ref, out_ref, w, give, mine, got, passing, last, w_sem, give_sem, got_sem, send_sem, recv_sem):
@@ -288,14 +417,6 @@
         product(dx, c, mine.at[b])
         return copy
 
-    def add(dst, a, b, rows):
-        step_r = min(16, rows)
-
-        @pl.loop(0, rows // step_r)
-        def _(i):
-            at = pl.ds(pl.multiple_of(i * step_r, step_r), step_r)
-            dst[at, :] = (a[at, :].astype(F32) + b[at, :].astype(F32)).astype(BF16)
-
     started = []
 
     def send(src, dst, device):
@@ -308,35 +429,28 @@
 
     pair = exchange(0, 2, True)
     pair.wait_recv()
-    add(mine.at[0], mine.at[0], got.at[0], block)
+    add_rows(mine.at[0], mine.at[0], got.at[0])
     pass_right = send(mine.at[0, h0], passing.at[0], right)
     pass_left = send(mine.at[0, h1], passing.at[1], left)
     pair_r = exchange(1, 1)
     pair_l = exchange(2, NX - 1)
     pair_r.wait_recv()
-    add(mine.at[1], mine.at[1], got.at[1], block)
+    add_rows(mine.at[1], mine.at[1], got.at[1])
     to_right_1 = send(mine.at[1, h1], last.at[0, h1], right)
     pair_l.wait_recv()
-    add(mine.at[2], mine.at[2], got.at[2], block)
+    add_rows(mine.at[2], mine.at[2], got.at[2])
     to_left_0 = send(mine.at[2, h0], last.at[1, h0], left)
     pair_o = exchange(3, 0)
     pass_right.wait_recv()
-    add(mine.at[1, h0], mine.at[1, h0], passing.at[0], half)
+    add_rows(mine.at[1, h0], mine.at[1, h0], passing.at[0])
     to_right_0 = send(mine.at[1, h0], last.at[0, h0], right)
     pass_left.wait_recv()
-    add(mine.at[2, h1], mine.at[2, h1], passing.at[1], half)
+    add_rows(mine.at[2, h1], mine.at[2, h1], passing.at[1])
     to_left_1 = send(mine.at[2, h1], last.at[1, h1], left)
     pair_o.wait_recv()
     for copy in (to_right_1, to_left_0, to_right_0, to_left_1):
         copy.wait_recv()
-    step_r = min(16, block)
-
-    @pl.loop(0, block // step_r)
-    def _(i):
-        at = pl.ds(pl.multiple_of(i * step_r, step_r), step_r)
-        total = (mine[3, at, :].astype(F32) + got[3, at, :].astype(F32)) + (last[0, at, :].astype(F32) + last[1, at, :].astype(F32))
-        out_ref[at, :] = (res_ref[at, :].astype(F32) + total.astype(BF16).astype(F32)).astype(BF16)
-
+    finish_rows(out_ref, res_ref, [mine.at[3], got.at[3], last.at[0], last.at[1]])
     for copy in (pair, pair_r, pair_l, pair_o, *started):
         copy.wait_send()
 
@@ -469,13 +583,17 @@
 
     def unit(q_row, k, v, masked):
         rows = pl.ds(pl.multiple_of(q_row, piece), piece)
-        for h in range(n_heads):
-            cols = slice(h * HD, (h + 1) * HD)
+        heads = [slice(h * HD, (h + 1) * HD) for h in range(n_heads)]
+
+        def score(cols):
             s = lax.dot_general(q_ref[rows, cols], k, (((1,), (1,)), ((), ())), preferred_element_type=F32) * scale
             if masked:
                 row = lax.broadcasted_iota(jnp.int32, (piece, piece), 0)
                 col = lax.broadcasted_iota(jnp.int32, (piece, piece), 1)
                 s = jnp.where(row >= col, s, -1e30)
+            return s
+
+        def absorb(cols, s):
             m_old = m_ref[rows, cols]
             m_new = jnp.maximum(m_old, jnp.max(s, axis=1, keepdims=True))
             alpha = jnp.exp2(m_old - m_new)
@@ -488,6 +606,11 @@
             pv = jnp.dot(pb, v, preferred_element_type=F32)
             acc_ref[rows, cols] = acc_ref[rows, cols] * alpha + pv
             m_ref[rows, cols] = m_new
+
+        ahead = score(heads[0])
+        for cols, after in zip(heads, heads[1:] + [None]):
+            s, ahead = ahead, score(after) if after else None
+            absorb(cols, s)
 
     @pl.loop(0, 2)
     def _(kind):
@@ -562,8 +685,7 @@
                            w_k.reshape(dim, HD), w_v.reshape(dim, HD), n_heads, piece)
         o = attention(q, kv)
         y_rows = scatter_product(o, w_o.reshape(n_heads * HD, dim), x_rows, 3)
-        hidden = gather_mlp_in(y_rows, g_mlp.reshape(1, dim), w_gate, w_up)
-        z_rows = scatter_product(hidden, w_down, y_rows, 4)
+        z_rows = mlp(y_rows, g_mlp.reshape(1, dim), w_gate, w_up, w_down)
         return z_rows[None]
 
     return jax.shard_map(local_layer, mesh=mesh,

time: 294 us -> 290 us (0.986)
  Pallas kernels: 283 us -> 274 us
  local copies, waits for them, and re-layouts: 8.53 us -> 13.1 us
    pallas_call x2 -> x1, Pallas kernels: 94.5 us -> 42.6 us  [scatter_product(): pl.pallas_call(scatter_kernel, out_shape=jax.ShapeDtypeStruct((block, dim...]
    pallas_call x1, Pallas kernels: 54.3 us -> 103 us  [mlp(): pl.pallas_call(mlp_kernel, out_shape=jax.ShapeDtypeStruct((block, dim), B...]
    pallas_call x1, Pallas kernels: 87.8 us -> 81.8 us  [attention(): pl.pallas_call(functools.partial(attention_kernel, width // HD), out_shap...]
    unnamed x20 -> x14, local copies, waits for them, and re-layouts: 7.91 us -> 11.8 us
where the time goes in v3:
time: 290 us
  Pallas kernels  274 us (94%)
  local copies, waits for them, and re-layouts  13.1 us (5%)
    pallas_call x1, Pallas kernels, mlp(): pl.pallas_call(mlp_kernel, out_shape=jax.ShapeDtypeStruct((block, dim), B...  103 us
    pallas_call x1, Pallas kernels, attention(): pl.pallas_call(functools.partial(attention_kernel, width // HD), out_shap...  81.8 us
    pallas_call x1, Pallas kernels, gather_qkv(): pl.pallas_call(functools.partial(qkv_kernel, n_heads), out_shape=(jax.Sha...  46.8 us
    pallas_call x1, Pallas kernels, scatter_product(): pl.pallas_call(scatter_kernel, out_shape=jax.ShapeDtypeStruct((block, dim...  42.6 us
    unnamed x14, local copies, waits for them, and re-layouts  11.8 us

profile of v3, /device:TPU:1, one launch (start us, length us, event | category | flops | bytes accessed | tf_op | source)
XLA Modules:
  0.0 289.8 jit_solution(8171286228146167376)
XLA Ops:
  0.0 1.9 fusion
  1.9 0.3 pad_maximum_fusion
  2.3 4.8 %copy.13 = bf16[512,8,4,128]{3,1,2,0:T(8,128)(2,1)} copy(bf16[512,8,4,128]{3,2,1,0:T(4,128)(2,1)} %bitcast.13) | data formatting | bytes 8388608
  7.1 0.7 reshape.34.g_ref
  7.8 0.0 copy-start
  7.8 1.2 copy-done
  9.1 0.0 copy-start.1
  9.1 1.2 copy-done.1
  10.3 0.0 copy-start.2
  10.3 1.2 copy-done.2
  11.5 46.8 %gather_qkv.1 = (bf16[1024,512]{1,0:T(8,128)(2,1)S(1)}, bf16[2,2,512,128]{3,2,1,0:T(8,128)(2,1)S(1)}) custom-call(bf16[128,4096]{1,0:T(8,128)(2,1)S(1)} %bitcast.11, bf16[1,4096]{1,0:T(2,128)(2,1)S(1)} %reshape.34.g_ref, f32[1024,128]{1,0:T(8,128)S(1)} %get-tuple-element.12.cos_ref, f32[1024,128]{1,0:T(8,128)S(1)} %get-tuple-element.13.sin_ref, ...), custom_call_target="tpu_custom_call" | custom-call | flops 6442450944 | bytes 6291456 | tf_op jit(solution)/shard_map/gather_qkv/pallas_call | solution.py:208
  58.3 0.0 copy-start.3
  58.4 81.8 %attention.1.h_ref = bf16[1024,512]{1,0:T(8,128)(2,1)S(1)} custom-call(bf16[1024,512]{1,0:T(8,128)(2,1)S(1)} %get-tuple-element.7.q_ref, bf16[2,2,512,128]{3,2,1,0:T(8,128)(2,1)S(1)} %get-tuple-element.8.kv_ref), custom_call_target="tpu_custom_call" | custom-call | flops 17999998976 | bytes 10485760 | tf_op jit(solution)/shard_map/attention/pallas_call | solution.py:657
  140.1 0.0 copy-start.5
  140.2 0.0 copy-done.3
  140.2 42.6 %scatter_product_3.1.y_hbm = bf16[128,4096]{1,0:T(8,128)(2,1)S(1)} custom-call(bf16[1024,512]{1,0:T(8,128)(2,1)S(1)} %attention.1.h_ref, bf16[512,4096]{1,0:T(8,128)(2,1)} %bitcast.16, bf16[128,4096]{1,0:T(8,128)(2,1)S(1)} %bitcast.12), custom_call_target="tpu_custom_call" | custom-call | flops 4294967296 | bytes 4194304 | tf_op jit(solution)/shard_map/scatter_product_3/pallas_call | solution.py:463
  182.7 0.0 copy-start.4
  182.7 1.0 copy-done.4
  183.7 0.0 copy-done.5
  183.7 0.6 reshape.39.g_ref
  184.3 103.2 %mlp.1 = bf16[128,4096]{1,0:T(8,128)(2,1)} custom-call(bf16[128,4096]{1,0:T(8,128)(2,1)} %copy-done.4, bf16[1,4096]{1,0:T(2,128)(2,1)} %reshape.39.g_ref, bf16[4096,1792]{1,0:T(8,128)(2,1)} %wg_hbm.1, bf16[4096,1792]{1,0:T(8,128)(2,1)} %wu_hbm.1, bf16[1792,4096]{1,0:T(8,128)(2,1)} %wd_hbm.1), custom_call_target="tpu_custom_call" | custom-call | flops 45097156608 | bytes 44040192 | tf_op jit(solution)/shard_map/mlp/pallas_call | solution.py:374
  287.6 2.3 copy.15
  (2 shorter events, 0.0 us)
Async XLA Ops:
  7.8 1.2 copy-start
  9.1 1.2 copy-start.1
  10.3 1.2 copy-start.2
  58.3 81.8 %copy-start.3 = (bf16[1,128,4096]{2,1,0:T(8,128)(2,1)S(1)}, bf16[1,128,4096]{2,1,0:T(8,128)(2,1)}, u32[]{:S(2)}) copy-start(bf16[1,128,4096]{2,1,0:T(8,128)(2,1)} %param.10) | copy-start | bytes 3145732
  140.1 43.6 %copy-start.5 = (bf16[4096]{0:T(1024)(128)(2,1)S(1)}, bf16[4096]{0:T(1024)(128)(2,1)}, u32[]{:S(2)}) copy-start(bf16[4096]{0:T(1024)(128)(2,1)} %param.16) | copy-start | bytes 24580
  182.7 1.0 copy-start.4
